TPU v7x, 32 devices: a whole 2x2x4 slice. The times are simulated.
32 devices in a mesh: gx: 8 (over z, x), gy: 4 (over y, core).
Axes of the slice: x: 2, y: 2, z: 4, core: 2. Of those that a mesh axis runs over, the one named last changes fastest.
Arguments:
- velocity: float32 [3, 8192, 512], P(None, ('gx', 'gy')), may hold values from -6 to 6
- positions: float32 [3, 1024, 256], P(None, ('gx', 'gy')), may hold values from -6 to 6
- stiff_h: float32 [1024, 256], P(('gx', 'gy')), may hold values from 0.1 to 1
- stiff_v: float32 [1024, 256], P(('gx', 'gy')), may hold values from 0.1 to 1
- marker_owner: int32 [262144, 1], P(('gx', 'gy')), may hold values from 0 to 31; in each aligned block of 8192 rows (0 to 8191, 8192 to 16383, ...) at most 384 rows name the same one
- marker_element: int32 [262144], P(('gx', 'gy')), may hold values from 0 to 255
- marker_coords: float32 [3, 262144], P(None, ('gx', 'gy')), may hold values from -1 to 1
Outputs:
- new_positions: float32 [3, 1024, 256], P(None, ('gx', 'gy'))
- node_forces: float32 [3, 8192, 512], P(None, ('gx', 'gy'))
Inputs may be any that keep to these rules, and one draw needn't show every extreme that they name: `marker_owner`: among the markers of one device's rows, no owner is named more than 384 times, and in some devices' rows one owner is named exactly 384 times.
All inputs are finite; a program needn't handle non-finite values.
Results may differ from a plain program's by a relative error of at most 0.00013.
Values sent between devices are 32-bit elements; how exact they have to be, the bound alone decides.
No kernel may reach another device: no remote copies, remote signals or barrier semaphores. Data moves between devices by JAX's collectives and lax.ppermute only.
A program may use at most 64 MiB of HBM per device.

v0:
```python
import math

import jax
import jax.numpy as jnp
from jax import lax
from jax.sharding import PartitionSpec as P

POINTS = 8


bend_modulus = 0.05
time_step = 0.5


def padded(cells, sides, width):
    for axis, dim in sides:
        count = lax.axis_size(axis)
        head = lax.slice_in_dim(cells, 0, width, axis=dim)
        tail = lax.slice_in_dim(cells, cells.shape[dim] - width, cells.shape[dim], axis=dim)
        cells = jnp.concatenate(
            [
                lax.ppermute(tail, axis, [(i, (i + 1) % count) for i in range(count)]),
                cells,
                lax.ppermute(head, axis, [((i + 1) % count, i) for i in range(count)]),
            ],
            axis=dim,
        )
    return cells


def basis(values):
    abscissa = -jnp.cos(jnp.pi * jnp.arange(POINTS).astype(values.dtype) / (POINTS - 1))
    collected = []
    for i in range(POINTS):
        product = jnp.ones_like(values)
        for j in range(POINTS):
            if j != i:
                product = product * ((values - abscissa[j]) / (abscissa[i] - abscissa[j]))
        collected.append(product)
    return jnp.stack(collected)


def weight_table(factors):
    along_r = factors[0:POINTS].T
    along_s = factors[POINTS : 2 * POINTS].T
    along_t = factors[2 * POINTS : 3 * POINTS].T
    table = along_r[:, :, None, None] * along_s[:, None, :, None] * along_t[:, None, None, :]
    return table.reshape(along_r.shape[0], POINTS * POINTS * POINTS)


def surface_laplacian(extended):
    middle = extended[:, 1:-1]
    return (
        extended[:, 2:]
        + extended[:, :-2]
        + jnp.roll(middle, 1, axis=2)
        + jnp.roll(middle, -1, axis=2)
        - 4.0 * middle
    )


def tension(extended, stiff_h):
    points = extended[:3]
    vertical = extended[3]
    middle = points[:, 1:-1]
    return (
        stiff_h * (jnp.roll(middle, -1, axis=2) - middle)
        + jnp.roll(stiff_h, 1, axis=1) * (jnp.roll(middle, 1, axis=2) - middle)
        + vertical[1:-1] * (points[:, 2:] - middle)
        + vertical[:-2] * (points[:, :-2] - middle)
    )


def three_factors(coords):
    return jnp.concatenate([basis(coords[0]), basis(coords[1]), basis(coords[2])], axis=0)


def selector_of(block_elements, elem_count):
    return (block_elements[:, None] == jnp.arange(elem_count, dtype=jnp.int32)[None, :]).astype(
        jnp.float32
    )


def local(velocity, positions, stiff_h, stiff_v, marker_owner, marker_element, marker_coords):
    major_count = lax.axis_size("gx")
    minor_count = lax.axis_size("gy")
    devices_all = major_count * minor_count
    marker_count = marker_owner.shape[0]
    capacity = 3 * marker_count // (2 * devices_all)
    slot_total = devices_all * capacity
    elem_count = velocity.shape[1]
    stacked = jnp.concatenate([positions, stiff_v[None]], axis=0)
    extended = padded(stacked, ((("gx", "gy"), 1),), 1)
    pulling = tension(extended, stiff_h)
    laplace = surface_laplacian(extended[:3])
    laplace_wide = padded(laplace, ((("gx", "gy"), 1),), 1)
    bending = -bend_modulus * surface_laplacian(laplace_wide)
    marker_force = (pulling + bending).reshape(3, marker_count)
    owners = marker_owner[:, 0]
    ordering = jnp.argsort(owners, stable=True)
    sorted_owners = owners[ordering]
    offsets = jnp.searchsorted(sorted_owners, jnp.arange(devices_all, dtype=jnp.int32), side="left")
    within = jnp.arange(marker_count, dtype=jnp.int32) - offsets[sorted_owners]
    places = (
        jnp.zeros((marker_count,), jnp.int32).at[ordering].set(sorted_owners * capacity + within)
    )
    described = three_factors(marker_coords)
    lead = described.shape[0]
    payload = jnp.concatenate([described, marker_force], axis=0)
    width_all = payload.shape[0]
    outgoing = jnp.zeros((width_all, slot_total), jnp.float32).at[:, places].set(payload)
    slot_ids = jnp.zeros((1, slot_total), jnp.int32).at[:, places].set(marker_element[None])
    got_floats, got_slots = (
        lax.all_to_all(
            lax.all_to_all(
                outgoing.reshape(width_all, major_count, minor_count, capacity),
                "gx",
                split_axis=1,
                concat_axis=1,
                tiled=True,
            ),
            "gy",
            split_axis=2,
            concat_axis=2,
            tiled=True,
        ),
        lax.all_to_all(
            lax.all_to_all(
                slot_ids.reshape(1, major_count, minor_count, capacity),
                "gx",
                split_axis=1,
                concat_axis=1,
                tiled=True,
            ),
            "gy",
            split_axis=2,
            concat_axis=2,
            tiled=True,
        ),
    )
    got_floats = got_floats.reshape(width_all, slot_total)
    element_ids = got_slots.reshape(slot_total)
    factors = got_floats[:lead]
    pushes = got_floats[lead:]
    block_len = math.gcd(slot_total, 512)
    block_count = slot_total // block_len
    factor_blocks = factors.reshape(3 * POINTS, block_count, block_len).transpose(1, 0, 2)
    element_blocks = element_ids.reshape(block_count, block_len)
    push_blocks = pushes.reshape(3, block_count, block_len).transpose(1, 0, 2)

    def sample(inputs):
        block_factors, block_elements = inputs
        weights = weight_table(block_factors)
        selector = selector_of(block_elements, elem_count)
        gathered = jnp.einsum("be,ken->kbn", selector, velocity, precision=lax.Precision.HIGHEST)
        return jnp.sum(gathered * weights[None], axis=-1)

    sampled = lax.map(sample, (factor_blocks, element_blocks))
    returning = sampled.transpose(1, 0, 2).reshape(3, slot_total)
    arrived = lax.all_to_all(
        lax.all_to_all(
            returning.reshape(3, major_count, minor_count, capacity),
            "gx",
            split_axis=1,
            concat_axis=1,
            tiled=True,
        ),
        "gy",
        split_axis=2,
        concat_axis=2,
        tiled=True,
    )

    def deposit(running, inputs):
        block_factors, block_elements, block_pushes = inputs
        weights = weight_table(block_factors)
        selector = selector_of(block_elements, elem_count)
        loads = block_pushes[:, :, None] * weights[None]
        added = jnp.einsum("be,kbn->ken", selector, loads, precision=lax.Precision.HIGHEST)
        return (running + added, None)

    node_forces, unused = lax.scan(
        deposit, jnp.zeros_like(velocity), (factor_blocks, element_blocks, push_blocks)
    )
    moved = jnp.take(arrived.reshape(3, slot_total), places, axis=1).reshape(positions.shape)
    return (positions + time_step * moved, node_forces)


def solution(mesh):
    return jax.shard_map(
        local,
        mesh=mesh,
        in_specs=(
            P(None, ("gx", "gy"), None),
            P(None, ("gx", "gy"), None),
            P(("gx", "gy"), None),
            P(("gx", "gy"), None),
            P(("gx", "gy"), None),
            P(("gx", "gy")),
            P(None, ("gx", "gy")),
        ),
        out_specs=(P(None, ("gx", "gy"), None), P(None, ("gx", "gy"), None)),
        check_vma=False,
    )
```

profile of v0, /device:TPU:0, one launch (start us, length us, event | category | flops | bytes accessed | tf_op | source)
XLA Modules:
  0.0 586.4 jit_solution(10198000036078593590)
XLA Ops:
  2.0 6.0 %collective-permute-start = (f32[4,1,256]{2,1,0:T(1,128)S(1)}, f32[4,1,256]{2,1,0:T(1,128)S(1)}, u32[]{:S(2)}, u32[]{:S(2)}) collective-permute-start(f32[4,1,256]{2,1,0:T(1,128)S(1)} %get-tuple-element.267), channel_id=1, source_target_pairs={{1,0},{2,1},{3,2},{4,3},{5,4},{6,5},{7,6},{8,7},{9,8},{10,9},{11,1... | collective-permute-start | bytes 12296 | tf_op jit(solution)/shard_map/ppermute | solution.py:24
  8.0 7.5 %sort.17 = (s32[8192]{0:T(1024)}, s32[8192]{0:T(1024)S(1)}) sort(s32[8192]{0:T(1024)} %bitcast.127, s32[8192]{0:T(1024)S(1)} %iota.23), dimensions={0}, to_apply=%region_0.1 | sort | flops 106496 | bytes 131072 | tf_op jit(solution)/shard_map/jit(argsort)/sort | solution.py:100
  15.5 45.5 %gather_fusion.1 = s32[8192]{0:T(1024)S(1)} fusion(s32[8192]{0:T(1024)S(1)} %bitcast.128, s32[8192]{0:T(1024)S(1)} %get-tuple-element.305), kind=kCustom, calls=%fused_computation.1 | custom fusion | bytes 98304 | tf_op jit(solution)/shard_map/gather | solution.py:101
  61.1 10.5 %while.46 = (s32[]{:T(128)}, u32[32]{0:T(128)S(1)}, u32[32]{0:T(128)S(1)}, s32[8192]{0:T(1024)S(1)}, s32[]{:T(128)}, /*index=5*/s32[]{:T(128)}, s32[]{}) while((s32[]{:T(128)}, u32[32]{0:T(128)S(1)}, u32[32]{0:T(128)S(1)}, s32[8192]{0:T(1024)S(1)}, s32[]{:T(128)}, /*index=5*/s32[]{:T(128)}, s32[]{}) %tuple.172), condition=%wide.region_2.3_spmd.clone, body=%wide.region_1.2_spmd.clone.sunk | while | flops 1444 | bytes 5732 | solution.py:102
  73.1 4.4 compare_select_fusion.1
  80.0 15.9 %fusion.35 = s32[8192]{0:T(1024)S(1)} fusion(pred[8192]{0:T(1024)(128)(4,1)S(1)} %get-tuple-element.228, pred[8192]{0:T(1024)(128)(4,1)S(1)} %get-tuple-element.227, pred[8192]{0:T(1024)(128)(4,1)S(1)} %get-tuple-element.226, pred[8192]{0:T(1024)(128)(4,1)S(1)} %get-tuple-element.225, pred[8192]{0:T(1024)(128)(4,1)S(1)} %get-tuple-element.224, ...), kind=kLoop, calls=%fused_computation.250 | loop fusion | flops 229376 | bytes 303204 | tf_op jit(solution)/shard_map/add | solution.py:105
  95.9 30.5 %scatter_custom_fusion = s32[8192]{0:T(1024)S(1)} fusion(s32[8192]{0:T(1024)S(1)} %get-tuple-element.306, s32[8192]{0:T(1024)S(1)} %fusion.35, s32[]{:T(128)} %constant.79.clone.1), kind=kCustom, calls=%fused_computation.280 | custom fusion | bytes 32772 | tf_op jit(solution)/shard_map/scatter | solution.py:105
  126.4 30.7 %scatter_custom_fusion.1 = s32[12288]{0:T(1024)S(1)} fusion(s32[8192]{0:T(1024)S(1)} %get-tuple-element.304, s32[8192]{0:T(1024)} %param.18, s32[]{:T(128)} %constant.79.clone.1), kind=kCustom, calls=%fused_computation.252 | custom fusion | bytes 49664 | tf_op jit(solution)/shard_map/scatter | solution.py:112
  157.8 3.5 all-to-all-start
  231.5 4.8 divide_multiply_fusion
  236.3 4.9 divide_multiply_fusion.6
  241.2 4.9 divide_multiply_fusion.12
  246.1 4.9 divide_multiply_fusion.18
  250.9 4.9 divide_multiply_fusion.24
  255.8 4.9 divide_multiply_fusion.30
  260.7 4.8 divide_multiply_fusion.36
  265.5 4.9 divide_multiply_fusion.42
  270.9 2.7 collective-permute-start.2
  274.9 5.3 collective-permute-done.3
  281.6 2.8 copy.89
  284.4 23.9 %scatter_custom_fusion.2 = f32[27,12288]{0,1:T(8,128)} fusion(s32[8192]{0:T(1024)S(1)} %get-tuple-element.304, f32[8192,27]{1,0:T(8,128)} %copy.89, f32[]{:T(128)} %constant.87.clone.1), kind=kCustom, calls=%fused_computation.41 | custom fusion | bytes 1327616 | tf_op jit(solution)/shard_map/scatter | solution.py:111
  308.2 5.5 copy.90
  313.8 3.6 all-to-all-start.2
  318.0 26.6 %all-to-all-done.2 = f32[27,8,4,384]{3,2,0,1:T(4,128)S(1)} async-done(((f32[27,8,4,384]{3,2,0,1:T(4,128)}), f32[27,8,4,384]{3,2,0,1:T(4,128)S(1)}, u32[]{:S(2)}, u32[]{:S(2)}) %all-to-all-start.2) | async-done | bytes 1327136 | tf_op jit(solution)/shard_map/all_to_all | solution.py:115
  344.6 3.8 all-to-all-start.1
  349.5 2.9 all-to-all-done.1
  352.4 4.5 all-to-all-start.3
  357.5 16.7 %all-to-all-done.3 = f32[27,8,4,384]{3,1,0,2:T(8,128)} async-done(((f32[27,8,4,384]{3,1,0,2:T(8,128)}), f32[27,8,4,384]{3,1,0,2:T(8,128)}, u32[]{:S(2)}, u32[]{:S(2)}) %all-to-all-start.3) | async-done | bytes 1327136 | tf_op jit(solution)/shard_map/all_to_all | solution.py:114
  377.9 3.0 copy.94
  380.9 64.9 %while.45 = (s32[]{:T(128)}, f32[24,3,512]{2,1,0:T(4,128)S(1)}, s32[24,512]{1,0:T(8,128)S(1)}, f32[3,256,512]{1,2,0:T(8,128)S(1)}, f32[24,24,512]{2,1,0:T(8,128)}, /*index=5*/s32[]{:T(128)}, s32[]{:T(128)}, s32[]{}, s32[]{}) while((s32[]{:T(128)}, f32[24,3,512]{2,1,0:T(4,128)S(1)}, s32[24,512]{1,0:T(8,128)S(1)}, f32[3,256,512]{1,2,0:T(8,128)S(1)}, ...), condition=%wide.region_8.9_spmd, body=%wide.region_6.8_spmd.sunk | while | flops 2417916416 | bytes 4108425 | solution.py:158
  446.6 3.8 all-to-all-start.4
  451.5 6.4 %all-to-all-done.4 = f32[3,8,4,384]{3,2,0,1:T(4,128)S(1)} async-done(((f32[3,8,4,384]{3,2,0,1:T(4,128)}), f32[3,8,4,384]{3,2,0,1:T(4,128)S(1)}, u32[]{:S(2)}, u32[]{:S(2)}) %all-to-all-start.4) | async-done | bytes 147488 | tf_op jit(solution)/shard_map/all_to_all | solution.py:161
  458.5 3.3 all-to-all-start.5
  461.8 85.0 %while.47 = (s32[]{:T(128)}, f32[3,256,512]{1,2,0:T(8,128)S(1)}, f32[24,3,512]{2,0,1:T(8,128)S(1)}, f32[24,24,512]{2,1,0:T(8,128)}, s32[24,512]{1,0:T(8,128)S(1)}, /*index=5*/s32[]{:T(128)}, s32[]{:T(128)}, s32[]{}, s32[]{}) while((s32[]{:T(128)}, f32[3,256,512]{1,2,0:T(8,128)S(1)}, f32[24,3,512]{2,0,1:T(8,128)S(1)}, ...), condition=%wide.region_10.11_spmd.clone, body=%wide.region_9.10_spmd.clone.sunk | while | flops 2417917952 | bytes 5689491 | solution.py:182
  473.5 2.5 bitcast_add_fusion.2
  480.5 2.5 bitcast_add_fusion.2
  487.6 2.5 bitcast_add_fusion.2
  494.7 2.5 bitcast_add_fusion.2
  501.8 2.5 bitcast_add_fusion.2
  508.9 2.5 bitcast_add_fusion.2
  516.0 2.5 bitcast_add_fusion.2
  523.0 2.5 bitcast_add_fusion.2
  530.1 2.5 bitcast_add_fusion.2
  537.2 2.5 bitcast_add_fusion.2
  544.3 2.5 bitcast_add_fusion.2
  548.5 4.0 copy.98
  552.4 30.5 %gather_fusion.2 = f32[8192,3]{1,0:T(8,128)} fusion(f32[3,12288]{0,1:T(8,128)} %bitcast.133, s32[8192]{0:T(1024)S(1)} %get-tuple-element.303), kind=kCustom, calls=%fused_computation.2 | custom fusion | bytes 229376 | tf_op jit(solution)/shard_map/jit(_take)/gather | solution.py:185
  582.9 2.8 copy.99
  (422 shorter events, 150.5 us)
Async XLA Ops:
  0.6 14.9 %copy-start = (s32[8192,1]{0,1:T(1,128)S(1)}, s32[8192,1]{0,1:T(1,128)}, u32[]{:S(2)}) copy-start(s32[8192,1]{0,1:T(1,128)} %param.17) | copy-start | bytes 98308
  1.4 269.1 %collective-permute-start.1 = (f32[4,1,256]{2,1,0:T(1,128)S(1)}, f32[4,1,256]{2,1,0:T(1,128)S(1)}, u32[]{:S(2)}, u32[]{:S(2)}) collective-permute-start(f32[4,1,256]{2,1,0:T(1,128)S(1)} %get-tuple-element.268), channel_id=1, source_target_pairs={{0,1},{1,2},{2,3},{3,4},{4,5},{5,6},{6,7},{7,8},{8,9},{9,10},{10,1... | collective-permute-start | bytes 12296 | tf_op jit(solution)/shard_map/ppermute | solution.py:22
  2.0 268.6 %collective-permute-start = (f32[4,1,256]{2,1,0:T(1,128)S(1)}, f32[4,1,256]{2,1,0:T(1,128)S(1)}, u32[]{:S(2)}, u32[]{:S(2)}) collective-permute-start(f32[4,1,256]{2,1,0:T(1,128)S(1)} %get-tuple-element.267), channel_id=1, source_target_pairs={{1,0},{2,1},{3,2},{4,3},{5,4},{6,5},{7,6},{8,7},{9,8},{10,9},{11,1... | collective-permute-start | bytes 12296 | tf_op jit(solution)/shard_map/ppermute | solution.py:24
  61.0 170.1 %copy-start.1 = (f32[3,32,256]{2,1,0:T(8,128)S(1)}, f32[3,32,256]{2,1,0:T(8,128)}, u32[]{:S(2)}) copy-start(f32[3,32,256]{2,1,0:T(8,128)} %param.14) | copy-start | bytes 294916
  71.6 159.8 %copy-start.5 = (f32[32,256]{1,0:T(8,128)S(1)}, f32[32,256]{1,0:T(8,128)}, u32[]{:S(2)}) copy-start(f32[32,256]{1,0:T(8,128)} %param.15) | copy-start | bytes 98308
  71.6 159.8 %copy-start.2 = (f32[3,8192]{1,0:T(4,128)S(1)}, f32[3,8192]{1,0:T(4,128)}, u32[]{:S(2)}) copy-start(f32[3,8192]{1,0:T(4,128)} %param.19) | copy-start | bytes 294916
  80.0 190.5 %copy-start.4 = (f32[32,256]{1,0:T(8,128)S(1)}, f32[32,256]{1,0:T(8,128)}, u32[]{:S(2)}) copy-start(f32[32,256]{1,0:T(8,128)} %param.16) | copy-start | bytes 98308
  157.8 156.0 %all-to-all-start = ((s32[1,8,4,384]{3,2,0,1:T(4,128)}), s32[1,8,4,384]{3,2,0,1:T(4,128)S(1)}, u32[]{:S(2)}, u32[]{:S(2)}) async-start(s32[1,8,4,384]{3,2,0,1:T(4,128)} %reshape.123), calls=%async_computation | async-start | bytes 98304 | tf_op jit(solution)/shard_map/all_to_all | solution.py:128
  270.9 4.0 collective-permute-start.2
  273.5 6.6 %collective-permute-start.3 = (f32[3,1,256]{2,1,0:T(1,128)S(1)}, f32[3,1,256]{2,1,0:T(1,128)S(1)}, u32[]{:S(2)}, u32[]{:S(2)}) collective-permute-start(f32[3,1,256]{2,1,0:T(1,128)S(1)} %get-tuple-element.298), channel_id=1, source_target_pairs={{0,1},{1,2},{2,3},{3,4},{4,5},{5,6},{6,7},{7,8},{8,9},{9,10},{10,1... | collective-permute-start | bytes 9224 | tf_op jit(solution)/shard_map/ppermute | solution.py:22
  313.8 30.8 %all-to-all-start.2 = ((f32[27,8,4,384]{3,2,0,1:T(4,128)}), f32[27,8,4,384]{3,2,0,1:T(4,128)S(1)}, u32[]{:S(2)}, u32[]{:S(2)}) async-start(f32[27,8,4,384]{3,2,0,1:T(4,128)} %copy.90), calls=%async_computation.2 | async-start | bytes 2654208 | tf_op jit(solution)/shard_map/all_to_all | solution.py:115
  344.6 7.8 %all-to-all-start.1 = ((s32[1,8,4,384]{3,1,0,2:T(8,128)}), s32[1,8,4,384]{3,1,0,2:T(8,128)S(1)}, u32[]{:S(2)}, u32[]{:S(2)}) async-start(s32[1,8,4,384]{3,1,0,2:T(8,128)} %copy.87), calls=%async_computation.1 | async-start | bytes 98304 | tf_op jit(solution)/shard_map/all_to_all | solution.py:127
  349.5 7.4 %copy-start.3 = (f32[3,256,512]{2,1,0:T(8,128)S(1)}, f32[3,256,512]{2,1,0:T(8,128)}, u32[]{:S(2)}) copy-start(f32[3,256,512]{2,1,0:T(8,128)} %param.13) | copy-start | bytes 4718596
  352.4 21.8 %all-to-all-start.3 = ((f32[27,8,4,384]{3,1,0,2:T(8,128)}), f32[27,8,4,384]{3,1,0,2:T(8,128)}, u32[]{:S(2)}, u32[]{:S(2)}) async-start(f32[27,8,4,384]{3,1,0,2:T(8,128)} %copy.91), calls=%async_computation.3 | async-start | bytes 2654208 | tf_op jit(solution)/shard_map/all_to_all | solution.py:114
  446.6 11.2 %all-to-all-start.4 = ((f32[3,8,4,384]{3,2,0,1:T(4,128)}), f32[3,8,4,384]{3,2,0,1:T(4,128)S(1)}, u32[]{:S(2)}, u32[]{:S(2)}) async-start(f32[3,8,4,384]{3,2,0,1:T(4,128)} %copy.96), calls=%async_computation.4 | async-start | bytes 294912 | tf_op jit(solution)/shard_map/all_to_all | solution.py:161
  458.5 90.0 %all-to-all-start.5 = ((f32[3,8,4,384]{3,1,0,2:T(8,128)}), f32[3,8,4,384]{3,1,0,2:T(8,128)S(1)}, u32[]{:S(2)}, u32[]{:S(2)}) async-start(f32[3,8,4,384]{3,1,0,2:T(8,128)} %copy.97), calls=%async_computation.5 | async-start | bytes 294912 | tf_op jit(solution)/shard_map/all_to_all | solution.py:160
where the time goes:
time: 596 us; the launch traced here: 586 us
  local copies, waits for them, and re-layouts  242 us (41%)
  matrix products  103 us (17%)
  other arithmetic  78.1 us (13%)
  between operations  70.2 us (12%)
  waiting for transfers between devices  59.2 us (10%)
  starting transfers between devices  31.7 us (5%)
    dot_general x24, matrix products, deposit(): jnp.einsum('be,kbn->ken', selector, loads, precision=lax.Precision.HIGHEST)  60.9 us
    gather x1, local copies, waits for them, and re-layouts, local(): sorted_owners = owners[ordering]  45.5 us
    dot_general x24, matrix products, sample(): jnp.einsum('be,ken->kbn', selector, velocity, precision=lax.Precision.HIG...  41.8 us
    mul x8, other arithmetic, basis(): product = product * ((values - abscissa[j]) / (abscissa[i] - abscissa[j]))  39 us
    transpose x48, local copies, waits for them, and re-layouts, weight_table(): along_r = factors[0:POINTS].T  36.7 us
    gather x2, local copies, waits for them, and re-layouts, local(): jnp.take(arrived.reshape(3, slot_total), places, axis=1)  33.3 us
    scatter x1, local copies, waits for them, and re-layouts, local(): jnp.zeros((1, slot_total), jnp.int32).at[:, places]  30.7 us
    scatter x1, local copies, waits for them, and re-layouts, local(): jnp.zeros((marker_count,), jnp.int32).at[ordering]  30.5 us
  transfers between devices with their start and end apart: 10, of which 6 were waited for; matrix products, arithmetic and copies ran while one was open for 53% of the time, Pallas kernels for 0%

commit v1 on v0

v1 whole, which is shorter than its diff:
```python
import math

import jax
import jax.numpy as jnp
import numpy as np
from jax import lax
from jax.experimental import pallas as pl
from jax.experimental.pallas import tpu as pltpu
from jax.sharding import PartitionSpec as P

POINTS = 8
NODES = POINTS * POINTS * POINTS
AXES = ("gx", "gy")
LANES = 256
GROUP = 32

bend_modulus = 0.05
time_step = 0.5

ABSCISSA = -np.cos(np.pi * np.arange(POINTS) / (POINTS - 1))
SCALE = np.array(
    [1.0 / np.prod([ABSCISSA[i] - ABSCISSA[j] for j in range(POINTS) if j != i]) for i in range(POINTS)]
)

NN = (((1,), (0,)), ((), ()))
NT = (((1,), (1,)), ((), ()))


def dot(a, b, dims):
    return lax.dot_general(a, b, dims, preferred_element_type=jnp.float32)


def split(x):
    high = x.astype(jnp.bfloat16).astype(jnp.float32)
    return high, x - high


def sublane(shape):
    return lax.broadcasted_iota(jnp.int32, shape, 0)


def halo(positions, stiff_v):
    count = lax.axis_size(AXES)
    tail = jnp.concatenate(
        [positions[:, -2], positions[:, -1], stiff_v[-1:]], axis=0
    )
    head = jnp.concatenate([positions[:, 0], positions[:, 1]], axis=0)
    above = lax.ppermute(tail, AXES, [(i, (i + 1) % count) for i in range(count)])
    below = lax.ppermute(head, AXES, [((i + 1) % count, i) for i in range(count)])
    wide = jnp.concatenate(
        [above[0:3][:, None], above[3:6][:, None], positions, below[0:3][:, None], below[3:6][:, None]], axis=1
    )
    vertical = jnp.concatenate([above[6:7], stiff_v], axis=0)
    return wide, vertical


def surface_laplacian(extended):
    middle = extended[:, 1:-1]
    return (
        extended[:, 2:]
        + extended[:, :-2]
        + jnp.roll(middle, 1, axis=2)
        + jnp.roll(middle, -1, axis=2)
        - 4.0 * middle
    )


def membrane_force(positions, stiff_h, stiff_v):
    wide, vertical = halo(positions, stiff_v)
    middle = positions
    pulling = (
        stiff_h * (jnp.roll(middle, -1, axis=2) - middle)
        + jnp.roll(stiff_h, 1, axis=1) * (jnp.roll(middle, 1, axis=2) - middle)
        + vertical[1:] * (wide[:, 3:-1] - middle)
        + vertical[:-1] * (wide[:, 1:-3] - middle)
    )
    return pulling - bend_modulus * surface_laplacian(surface_laplacian(wide))


def one_hot(count, centred):
    shape = (count, centred.shape[1])
    row = (sublane(shape) - count // 2).astype(jnp.bfloat16)
    return jnp.where(row == centred, jnp.bfloat16(1), jnp.bfloat16(0))


def pack_kernel(owner_ref, element_ref, coords_ref, force_ref, out_ref, rank_ref, base_ref, acc_ref):
    owners, _, capacity = out_ref.shape
    markers = owner_ref.shape[1]
    row = lax.broadcasted_iota(jnp.int32, (LANES, LANES), 0)
    col = lax.broadcasted_iota(jnp.int32, (LANES, LANES), 1)
    before = jnp.where(row < col, 1.0, 0.0).astype(jnp.bfloat16)
    base_ref[...] = jnp.zeros_like(base_ref)
    acc_ref[...] = jnp.zeros_like(acc_ref)

    def ranks(r, carry):
        at = pl.ds(pl.multiple_of(r * LANES, LANES), LANES)
        own = owner_ref[:, at]
        hot = jnp.where(sublane((owners, LANES)) == own, 1.0, 0.0)
        earlier = dot(hot.astype(jnp.bfloat16), before, NN) + base_ref[...]
        rank_ref[:, at] = jnp.sum(hot * earlier, axis=0, keepdims=True).astype(jnp.int32)
        base_ref[...] = base_ref[...] + jnp.sum(hot, axis=1, keepdims=True)
        return carry

    lax.fori_loop(0, markers // LANES, ranks, 0, unroll=8)
    rows = force_ref.shape[2]
    step = 2 * rows

    def route(r, carry):
        at = pl.ds(pl.multiple_of(r * step, step), step)
        own = jnp.broadcast_to(owner_ref[:, at].astype(jnp.float32), (16, step)).astype(jnp.bfloat16)
        rank = (rank_ref[:, at] - capacity // 2).astype(jnp.float32).astype(jnp.bfloat16)
        force = [
            jnp.concatenate([force_ref[k, pl.ds(2 * r, 1), :], force_ref[k, pl.ds(2 * r + 1, 1), :]], axis=1)
            for k in range(3)
        ]
        payload = jnp.concatenate(
            [
                coords_ref[:, at],
                *force,
                element_ref[:, at].astype(jnp.float32) + 1.0,
                jnp.zeros((1, step), jnp.float32),
            ],
            axis=0,
        )
        both = jnp.concatenate(split(payload), axis=0).astype(jnp.bfloat16)
        left = jnp.concatenate(
            [jnp.where(own == jnp.bfloat16(d), both, jnp.bfloat16(0)) for d in range(owners)], axis=0
        )
        acc_ref[...] += dot(left, one_hot(capacity, rank), NT)
        return carry

    lax.fori_loop(0, markers // step, route, 0)
    for d in range(owners):
        out_ref[d] = acc_ref[16 * d : 16 * d + 8] + acc_ref[16 * d + 8 : 16 * d + 16]


def place_kernel(got_ref, place_ref, range_ref, hot_ref):
    sources, _, capacity = got_ref.shape
    groups = range_ref.shape[0]
    row = lax.broadcasted_iota(jnp.int32, (capacity, capacity), 0)
    col = lax.broadcasted_iota(jnp.int32, (capacity, capacity), 1)
    before = jnp.where(row < col, 1.0, 0.0).astype(jnp.bfloat16)
    kind = sublane((groups, capacity)).astype(jnp.float32)
    for s in range(sources):
        group = jnp.floor((got_ref[s, 6:7, :] - 1.0) * (1.0 / GROUP))
        hot_ref[s * groups : (s + 1) * groups, :] = jnp.where(kind == group, 1.0, 0.0)
    earlier = dot(hot_ref[...].astype(jnp.bfloat16), before, NN)
    count = jnp.sum(hot_ref[...], axis=1, keepdims=True)
    total = jnp.zeros((groups, 1), jnp.float32)
    for s in range(sources):
        total = total + count[s * groups : (s + 1) * groups]
    start = jnp.zeros((groups, 1), jnp.float32)
    for g in range(groups):
        start = start + jnp.where(sublane((groups, 1)) > g, total[g : g + 1], 0.0)
    base = start + 1.0
    for s in range(sources):
        rows = slice(s * groups, (s + 1) * groups)
        spot = jnp.sum(hot_ref[rows, :] * (earlier[rows] + base), axis=0, keepdims=True) - 1.0
        place_ref[s : s + 1, :] = spot
        base = base + count[rows]
    edge = (lax.broadcasted_iota(jnp.int32, range_ref.shape, 1) * LANES).astype(jnp.float32)
    first = jnp.sum(jnp.where(start + total <= edge, 1.0, 0.0), axis=0, keepdims=True)
    first = jnp.minimum(first, groups - 1.0)
    last = jnp.sum(jnp.where(start < edge + LANES, 1.0, 0.0), axis=0, keepdims=True)
    filled = jnp.sum(total, axis=0, keepdims=True)
    used = jnp.floor((filled + (LANES - 1)) * (1.0 / LANES)) + jnp.zeros_like(first)
    which = sublane(range_ref.shape)
    range_ref[...] = jnp.where(which == 0, first, jnp.where(which == 1, last, used)).astype(jnp.int32)


def spots(place_ref, i, per):
    spot = jnp.concatenate([place_ref[pl.ds(i * per + j, 1), :] for j in range(per)], axis=1)
    high = jnp.floor(spot * (1.0 / LANES))
    return high, (spot - high * LANES - LANES // 2).astype(jnp.bfloat16)


def sort_kernel(got_ref, place_ref, out_ref, acc_ref):
    sources, _, capacity = got_ref.shape
    chunks = out_ref.shape[0]
    per = 2
    acc_ref[...] = jnp.zeros_like(acc_ref)

    def gather(i, carry):
        payload = jnp.concatenate([got_ref[i * per + j] for j in range(per)], axis=1)
        both = jnp.concatenate(split(payload), axis=0).astype(jnp.bfloat16)
        high, low = spots(place_ref, i, per)
        high = jnp.broadcast_to(high, (16, per * capacity)).astype(jnp.bfloat16)
        left = jnp.concatenate(
            [jnp.where(high == jnp.bfloat16(h), both, jnp.bfloat16(0)) for h in range(chunks)], axis=0
        )
        acc_ref[...] += dot(left, one_hot(LANES, low), NT)
        return carry

    lax.fori_loop(0, sources // per, gather, 0)
    for h in range(chunks):
        out_ref[h] = acc_ref[16 * h : 16 * h + 8] + acc_ref[16 * h + 8 : 16 * h + 16]


def return_kernel(place_ref, sampled_ref, out_ref):
    sources, _, capacity = out_ref.shape
    chunks = sampled_ref.shape[0]
    per = 2
    rows = []
    for h in range(chunks):
        rows.extend(split(sampled_ref[h]))
    table = jnp.concatenate(rows, axis=0).astype(jnp.bfloat16)

    def scatter(i, carry):
        high, low = spots(place_ref, i, per)
        high = jnp.broadcast_to(high, (8, per * capacity))
        picked = dot(table, one_hot(LANES, low), NN)
        total = jnp.zeros((8, per * capacity), jnp.float32)
        for h in range(chunks):
            total = total + jnp.where(high == float(h), picked[8 * h : 8 * h + 8], 0.0)
        total = total[0:4] + total[4:8]
        for j in range(per):
            out_ref[i * per + j] = total[:, j * capacity : (j + 1) * capacity]
        return carry

    lax.fori_loop(0, sources // per, scatter, 0)


def basis_rows(x):
    node = sublane((POINTS, x.shape[1]))
    value = jnp.zeros((POINTS, x.shape[1]), jnp.float32)
    for i in range(POINTS):
        value = jnp.where(node == i, float(SCALE[i]), value)
    for j in range(POINTS):
        value = value * jnp.where(node == j, 1.0, x - float(ABSCISSA[j]))
    return value


def build_weights(payload, weight_ref):
    along_r = basis_rows(payload[0:1])
    along_s = basis_rows(payload[1:2])
    along_t = basis_rows(payload[2:3])
    plane = jnp.concatenate([along_s[b : b + 1] * along_t for b in range(POINTS)], axis=0)
    step = POINTS * POINTS
    for a in range(POINTS):
        block = along_r[a : a + 1] * plane
        high = block.astype(jnp.bfloat16)
        weight_ref[0, a * step : (a + 1) * step, :] = high
        weight_ref[1, a * step : (a + 1) * step, :] = (block - high.astype(jnp.float32)).astype(jnp.bfloat16)


def prepare_kernel(velocity_ref, out_ref):
    groups = out_ref.shape[0]
    for g in range(groups):
        for k in range(3):
            high, low = split(velocity_ref[k, g * GROUP : (g + 1) * GROUP, :])
            out_ref[g, k * GROUP : (k + 1) * GROUP, :] = high.astype(jnp.bfloat16)
            out_ref[g, (3 + k) * GROUP : (4 + k) * GROUP, :] = low.astype(jnp.bfloat16)


def hot_elements(payload, g):
    return jnp.where(
        sublane((GROUP, LANES)).astype(jnp.float32) + (g * GROUP + 1).astype(jnp.float32) == payload[6:7], 1.0, 0.0
    )


def sample_kernel(range_ref, sorted_ref, velocity_ref, out_ref, even_ref, odd_ref):
    used = range_ref[2, 0]
    out_ref[...] = jnp.zeros_like(out_ref)

    def visit(c, g, weight_ref):
        wide = dot(velocity_ref[g], weight_ref[0], NN)
        narrow = dot(velocity_ref[g, 0 : 3 * GROUP], weight_ref[1], NN)
        total = wide[: 3 * GROUP] + wide[3 * GROUP :] + narrow
        hot = hot_elements(sorted_ref[c], g)
        sums = [jnp.sum(hot * total[k * GROUP : (k + 1) * GROUP], axis=0, keepdims=True) for k in range(3)]
        out_ref[c] += jnp.concatenate(sums + [jnp.zeros((1, LANES), jnp.float32)], axis=0)

    pipeline(range_ref, used, visit, sorted_ref, even_ref, odd_ref)


def pipeline(range_ref, used, visit, sorted_ref, even_ref, odd_ref):
    last = sorted_ref.shape[0] - 1
    build_weights(sorted_ref[0], even_ref)

    def half(c, this_ref, next_ref):
        visit(c, range_ref[0, c], this_ref)
        build_weights(sorted_ref[jnp.minimum(c + 1, last)], next_ref)

        def more(g, carry):
            visit(c, g, this_ref)
            return carry

        lax.fori_loop(range_ref[0, c] + 1, range_ref[1, c], more, 0)

    def pair(i, carry):
        half(2 * i, even_ref, odd_ref)
        half(2 * i + 1, odd_ref, even_ref)
        return carry

    lax.fori_loop(0, (used + 1) // 2, pair, 0)


def deposit_kernel(range_ref, sorted_ref, out_ref, even_ref, odd_ref):
    used = range_ref[2, 0]
    out_ref[...] = jnp.zeros_like(out_ref)

    def visit(c, g, weight_ref):
        payload = sorted_ref[c]
        hot = hot_elements(payload, g)
        high, low = split(payload)
        left = jnp.concatenate(
            [hot * part[3 + k : 4 + k] for part in (high, low) for k in range(3)], axis=0
        ).astype(jnp.bfloat16)
        wide = dot(left, weight_ref[0], NT)
        narrow = dot(left[: 3 * GROUP], weight_ref[1], NT)
        total = wide[: 3 * GROUP] + wide[3 * GROUP :] + narrow
        rows = pl.ds(pl.multiple_of(g * GROUP, GROUP), GROUP)
        for k in range(3):
            out_ref[k, rows, :] += total[k * GROUP : (k + 1) * GROUP]

    pipeline(range_ref, used, visit, sorted_ref, even_ref, odd_ref)


def unpack_kernel(owner_ref, rank_ref, arrived_ref, positions_ref, out_ref):
    owners, _, capacity = arrived_ref.shape
    chunks = owner_ref.shape[1] // LANES
    rows = []
    for d in range(owners):
        rows.extend(split(arrived_ref[d]))
    table = jnp.concatenate(rows, axis=0).astype(jnp.bfloat16)

    def chunk(r, carry):
        at = pl.ds(pl.multiple_of(r * LANES, LANES), LANES)
        own = jnp.broadcast_to(owner_ref[:, at], (8, LANES))
        rank = (rank_ref[:, at] - capacity // 2).astype(jnp.float32).astype(jnp.bfloat16)
        picked = dot(table, one_hot(capacity, rank), NN)
        total = jnp.zeros((8, LANES), jnp.float32)
        for d in range(owners):
            total = total + jnp.where(own == d, picked[8 * d : 8 * d + 8], 0.0)
        for k in range(3):
            moved = total[k : k + 1] + total[4 + k : 5 + k]
            out_ref[k, pl.ds(r, 1), :] = positions_ref[k, pl.ds(r, 1), :] + time_step * moved
        return carry

    lax.fori_loop(0, chunks, chunk, 0, unroll=2)


def exchange(x):
    return lax.all_to_all(x, AXES, 0, 0, tiled=True)


def local(velocity, positions, stiff_h, stiff_v, marker_owner, marker_element, marker_coords):
    devices = lax.axis_size(AXES)
    markers = marker_owner.shape[0]
    capacity = 3 * markers // (2 * devices)
    slots = devices * capacity
    elements = velocity.shape[1]
    groups = elements // GROUP
    f32 = jnp.float32

    force = membrane_force(positions, stiff_h, stiff_v)
    owner = marker_owner.reshape(1, markers)
    element = marker_element.reshape(1, markers)
    outgoing, rank = pl.pallas_call(
        pack_kernel,
        out_shape=(
            jax.ShapeDtypeStruct((devices, 8, capacity), f32),
            jax.ShapeDtypeStruct((1, markers), jnp.int32),
        ),
        scratch_shapes=[pltpu.VMEM((devices, 1), f32), pltpu.VMEM((devices * 16, capacity), f32)],
        name="pack",
    )(owner, element, marker_coords, force)
    got = exchange(outgoing)
    table = pl.pallas_call(
        prepare_kernel,
        out_shape=jax.ShapeDtypeStruct((groups, 6 * GROUP, NODES), jnp.bfloat16),
        name="prepare",
    )(velocity)
    chunks = slots // LANES
    place, spans = pl.pallas_call(
        place_kernel,
        out_shape=(
            jax.ShapeDtypeStruct((devices, capacity), f32),
            jax.ShapeDtypeStruct((groups, 128), jnp.int32),
        ),
        scratch_shapes=[pltpu.VMEM((devices * groups, capacity), f32)],
        name="place",
    )(got)
    ordered = pl.pallas_call(
        sort_kernel,
        out_shape=jax.ShapeDtypeStruct((chunks, 8, LANES), f32),
        scratch_shapes=[pltpu.VMEM((chunks * 16, LANES), f32)],
        name="sort",
    )(got, place)
    weights = pltpu.VMEM((2, NODES, LANES), jnp.bfloat16)
    scalars = pl.BlockSpec(memory_space=pltpu.SMEM)
    vector = pl.BlockSpec(memory_space=pltpu.VMEM)
    sampled = pl.pallas_call(
        sample_kernel,
        out_shape=jax.ShapeDtypeStruct((chunks, 4, LANES), f32),
        in_specs=[scalars, vector, vector],
        scratch_shapes=[weights, weights],
        name="sample",
    )(spans, ordered, table)
    returning = pl.pallas_call(
        return_kernel,
        out_shape=jax.ShapeDtypeStruct((devices, 4, capacity), f32),
        name="return",
    )(place, sampled)
    arrived = exchange(returning)
    node_forces = pl.pallas_call(
        deposit_kernel,
        out_shape=jax.ShapeDtypeStruct(velocity.shape, f32),
        in_specs=[scalars, vector],
        scratch_shapes=[weights, weights],
        name="deposit",
    )(spans, ordered)
    moved = pl.pallas_call(
        unpack_kernel,
        out_shape=jax.ShapeDtypeStruct(positions.shape, f32),
        name="unpack",
    )(owner, rank, arrived, positions)
    return moved, node_forces


def solution(mesh):
    return jax.shard_map(
        local,
        mesh=mesh,
        in_specs=(
            P(None, AXES, None),
            P(None, AXES, None),
            P(AXES, None),
            P(AXES, None),
            P(AXES, None),
            P(AXES),
            P(None, AXES),
        ),
        out_specs=(P(None, AXES, None), P(None, AXES, None)),
        check_vma=False,
    )
```

time: 596 us -> 113 us (0.19)
  the two profiles are of different devices: /device:TPU:0 before, /device:TPU:3 now
where the time goes in v1:
time: 113 us
  Pallas kernels  78.8 us (70%)
  starting transfers between devices  15.4 us (14%)
  waiting for transfers between devices  8.97 us (8%)
  local copies, waits for them, and re-layouts  6.12 us (5%)
  other arithmetic  2.71 us (2%)
    pallas_call x1, Pallas kernels, local(): pl.pallas_call(deposit_kernel, out_shape=jax.ShapeDtypeStruct(velocity.sh...  21.2 us
    pallas_call x1, Pallas kernels, local(): pl.pallas_call(sample_kernel, out_shape=jax.ShapeDtypeStruct((chunks, 4,...  17.8 us
    all_to_all x2, starting transfers between devices, exchange(): return lax.all_to_all(x, AXES, 0, 0, tiled=True)  13.4 us
    pallas_call x1, Pallas kernels, local(): pl.pallas_call(pack_kernel, out_shape=(jax.ShapeDtypeStruct((devices, 8,...  10.9 us
    pallas_call x1, Pallas kernels, local(): pl.pallas_call(sort_kernel, out_shape=jax.ShapeDtypeStruct((chunks, 8, LA...  10.2 us
    all_to_all x2, waiting for transfers between devices, exchange(): return lax.all_to_all(x, AXES, 0, 0, tiled=True)  8.96 us
    pallas_call x1, Pallas kernels, local(): pl.pallas_call(return_kernel, out_shape=jax.ShapeDtypeStruct((devices, 4,...  7.1 us
    pallas_call x1, Pallas kernels, local(): pl.pallas_call(unpack_kernel, out_shape=jax.ShapeDtypeStruct(positions.sh...  6.87 us
  transfers between devices with their start and end apart: 4, of which 1 were waited for; matrix products, arithmetic and copies ran while one was open for 4% of the time, Pallas kernels for 21%

profile of v1, /device:TPU:3, one launch (start us, length us, event | category | flops | bytes accessed | tf_op | source)
XLA Modules:
  0.0 112.7 jit_solution(7840694972647045875)
XLA Ops:
  0.6 0.0 copy-start
  0.6 0.0 copy-start.4
  0.7 0.0 copy-start.3
  0.7 0.9 fusion.23
  1.6 0.7 collective-permute-start
  2.3 0.7 slice.125
  3.0 1.2 %collective-permute-start.1 = (f32[7,256]{1,0:T(8,128)S(1)}, f32[7,256]{1,0:T(8,128)S(1)}, u32[]{:S(2)}, u32[]{:S(2)}) collective-permute-start(f32[7,256]{1,0:T(8,128)S(1)} %pad_maximum_fusion.6), channel_id=1, source_target_pairs={{0,1},{1,2},{2,3},{3,4},{4,5},{5,6},{6,7},{7,8},{8,9},{9,10},{10,1... | collective-permute-start | bytes 21512 | tf_op jit(solution)/shard_map/ppermute | solution.py:48
  4.2 0.9 fusion.21
  5.1 1.1 fusion.22
  6.2 0.8 slice.115
  7.0 0.8 pad_maximum_fusion.4
  7.8 0.0 collective-permute-done
  7.8 0.0 collective-permute-done.1
  7.9 0.9 pad_maximum_fusion
  8.8 0.1 fusion.19
  8.9 0.1 fusion.20
  9.0 0.0 copy-done
  9.0 0.1 fusion.2
  9.1 0.1 fusion.17
  9.2 0.1 fusion.18
  9.3 0.0 copy-done.4
  9.3 0.0 copy-done.3
  9.3 0.8 fusion.5.force_ref
  10.1 10.9 %pack.1 = (f32[32,8,384]{2,1,0:T(8,128)}, s32[1,8192]{1,0:T(1,128)}) custom-call(s32[1,8192]{1,0:T(1,128)} %bitcast.16, s32[1,8192]{1,0:T(1,128)} %bitcast.18, f32[3,8192]{1,0:T(4,128)} %coords_ref.1, f32[3,32,256]{2,1,0:T(8,128)} %fusion.5.force_ref), custom_call_target="tpu_custom_call" | custom-call | tf_op jit(solution)/shard_map/pack/pallas_call | solution.py:359
  21.0 9.4 %all-to-all-start = ((f32[32,8,384]{2,1,0:T(8,128)}), f32[32,8,384]{2,1,0:T(8,128)S(1)}, u32[]{:S(2)}, u32[]{:S(2)}) async-start(f32[32,8,384]{2,1,0:T(8,128)} %get-tuple-element.7), calls=%async_computation | async-start | bytes 786432 | tf_op jit(solution)/shard_map/all_to_all | solution.py:344
  30.4 2.7 %prepare.1.velocity_ref = bf16[8,192,512]{2,1,0:T(8,128)(2,1)} custom-call(f32[3,256,512]{2,1,0:T(8,128)} %velocity_ref.1), custom_call_target="tpu_custom_call" | custom-call | tf_op jit(solution)/shard_map/prepare/pallas_call | solution.py:369
  33.1 9.0 %all-to-all-done.got_ref = f32[32,8,384]{2,1,0:T(8,128)S(1)} async-done(((f32[32,8,384]{2,1,0:T(8,128)}), f32[32,8,384]{2,1,0:T(8,128)S(1)}, u32[]{:S(2)}, u32[]{:S(2)}) %all-to-all-start) | async-done | bytes 393248 | tf_op jit(solution)/shard_map/all_to_all | solution.py:344
  42.1 0.0 copy-start.1
  42.1 0.7 copy-done.1
  42.8 2.0 %place.1 = (f32[32,384]{1,0:T(8,128)}, s32[8,128]{1,0:T(8,128)}) custom-call(f32[32,8,384]{2,1,0:T(8,128)} %copy-done.1), custom_call_target="tpu_custom_call" | custom-call | tf_op jit(solution)/shard_map/place/pallas_call | solution.py:375
  44.8 10.2 %sort.1.sorted_ref = f32[48,8,256]{2,1,0:T(8,128)} custom-call(f32[32,8,384]{2,1,0:T(8,128)} %copy-done.1, f32[32,384]{1,0:T(8,128)} %get-tuple-element.8.place_ref), custom_call_target="tpu_custom_call" | custom-call | tf_op jit(solution)/shard_map/sort/pallas_call | solution.py:384
  55.0 17.8 %sample.1.sampled_ref = f32[48,4,256]{2,1,0:T(4,128)} custom-call(s32[8,128]{1,0:T(8,128)} %get-tuple-element.9.range_ref, f32[48,8,256]{2,1,0:T(8,128)} %sort.1.sorted_ref, bf16[8,192,512]{2,1,0:T(8,128)(2,1)} %prepare.1.velocity_ref), custom_call_target="tpu_custom_call" | custom-call | tf_op jit(solution)/shard_map/sample/pallas_call | solution.py:393
  72.8 7.1 %return.1 = f32[32,4,384]{2,1,0:T(4,128)} custom-call(f32[32,384]{1,0:T(8,128)} %get-tuple-element.8.place_ref, f32[48,4,256]{2,1,0:T(4,128)} %sample.1.sampled_ref), custom_call_target="tpu_custom_call" | custom-call | tf_op jit(solution)/shard_map/return/pallas_call | solution.py:400
  79.9 4.1 %all-to-all-start.1 = ((f32[32,4,384]{2,1,0:T(4,128)}), f32[32,4,384]{2,1,0:T(4,128)S(1)}, u32[]{:S(2)}, u32[]{:S(2)}) async-start(f32[32,4,384]{2,1,0:T(4,128)} %return.1), calls=%async_computation.1 | async-start | bytes 393216 | tf_op jit(solution)/shard_map/all_to_all | solution.py:344
  84.0 21.2 %deposit.1 = f32[3,256,512]{2,1,0:T(8,128)} custom-call(s32[8,128]{1,0:T(8,128)} %get-tuple-element.9.range_ref, f32[48,8,256]{2,1,0:T(8,128)} %sort.1.sorted_ref), custom_call_target="tpu_custom_call" | custom-call | tf_op jit(solution)/shard_map/deposit/pallas_call | solution.py:406
  105.2 0.0 all-to-all-done.1.arrived_ref
  105.2 0.0 copy-start.2
  105.2 0.7 copy-done.2
  105.8 6.9 %unpack.1 = f32[3,32,256]{2,1,0:T(8,128)} custom-call(s32[1,8192]{1,0:T(1,128)} %bitcast.17, s32[1,8192]{1,0:T(1,128)} %get-tuple-element.6.rank_ref, f32[32,4,384]{2,1,0:T(4,128)} %copy-done.2, f32[3,32,256]{2,1,0:T(8,128)} %positions_ref.1), custom_call_target="tpu_custom_call" | custom-call | tf_op jit(solution)/shard_map/unpack/pallas_call | solution.py:413
  (12 shorter events, 0.1 us)
Async XLA Ops:
  0.6 8.3 %copy-start = (f32[3,32,256]{2,1,0:T(8,128)S(1)}, f32[3,32,256]{2,1,0:T(8,128)}, u32[]{:S(2)}) copy-start(f32[3,32,256]{2,1,0:T(8,128)} %positions_ref.1) | copy-start | bytes 294916
  0.6 8.7 %copy-start.4 = (f32[32,256]{1,0:T(8,128)S(1)}, f32[32,256]{1,0:T(8,128)}, u32[]{:S(2)}) copy-start(f32[32,256]{1,0:T(8,128)} %param.10) | copy-start | bytes 98308
  0.7 8.7 %copy-start.3 = (f32[32,256]{1,0:T(8,128)S(1)}, f32[32,256]{1,0:T(8,128)}, u32[]{:S(2)}) copy-start(f32[32,256]{1,0:T(8,128)} %param.9) | copy-start | bytes 98308
  1.6 6.2 %collective-permute-start = (f32[6,256]{1,0:T(8,128)S(1)}, f32[6,256]{1,0:T(8,128)S(1)}, u32[]{:S(2)}, u32[]{:S(2)}) collective-permute-start(f32[6,256]{1,0:T(8,128)S(1)} %pad_maximum_fusion.5), channel_id=1, source_target_pairs={{1,0},{2,1},{3,2},{4,3},{5,4},{6,5},{7,6},{8,7},{9,8},{10,9},{11,1... | collective-permute-start | bytes 18440 | tf_op jit(solution)/shard_map/ppermute | solution.py:49
  3.0 4.8 %collective-permute-start.1 = (f32[7,256]{1,0:T(8,128)S(1)}, f32[7,256]{1,0:T(8,128)S(1)}, u32[]{:S(2)}, u32[]{:S(2)}) collective-permute-start(f32[7,256]{1,0:T(8,128)S(1)} %pad_maximum_fusion.6), channel_id=1, source_target_pairs={{0,1},{1,2},{2,3},{3,4},{4,5},{5,6},{6,7},{7,8},{8,9},{9,10},{10,1... | collective-permute-start | bytes 21512 | tf_op jit(solution)/shard_map/ppermute | solution.py:48
  21.0 21.1 %all-to-all-start = ((f32[32,8,384]{2,1,0:T(8,128)}), f32[32,8,384]{2,1,0:T(8,128)S(1)}, u32[]{:S(2)}, u32[]{:S(2)}) async-start(f32[32,8,384]{2,1,0:T(8,128)} %get-tuple-element.7), calls=%async_computation | async-start | bytes 786432 | tf_op jit(solution)/shard_map/all_to_all | solution.py:344
  42.1 0.7 copy-start.1
  79.9 25.3 %all-to-all-start.1 = ((f32[32,4,384]{2,1,0:T(4,128)}), f32[32,4,384]{2,1,0:T(4,128)S(1)}, u32[]{:S(2)}, u32[]{:S(2)}) async-start(f32[32,4,384]{2,1,0:T(4,128)} %return.1), calls=%async_computation.1 | async-start | bytes 393216 | tf_op jit(solution)/shard_map/all_to_all | solution.py:344
  105.2 0.7 copy-start.2

commit v2 on v1

v2 whole, which is shorter than its diff:
```python
import functools

import jax
import jax.numpy as jnp
import numpy as np
from jax import lax
from jax.experimental import pallas as pl
from jax.experimental.pallas import tpu as pltpu
from jax.sharding import PartitionSpec as P

POINTS = 8
NODES = POINTS * POINTS * POINTS
AXES = ("gx", "gy")
SMALL = pltpu.CompilerParams(vmem_limit_bytes=20 * 1024 * 1024)
LANES = 256
GROUP = 32
DEPTH = 4

bend_modulus = 0.05
time_step = 0.5

ABSCISSA = -np.cos(np.pi * np.arange(POINTS) / (POINTS - 1))
SCALE = np.array(
    [1.0 / np.prod([ABSCISSA[i] - ABSCISSA[j] for j in range(POINTS) if j != i]) for i in range(POINTS)]
)

NN = (((1,), (0,)), ((), ()))
NT = (((1,), (1,)), ((), ()))


def dot(a, b, dims):
    return lax.dot_general(a, b, dims, preferred_element_type=jnp.float32)


def split(x):
    high = x.astype(jnp.bfloat16).astype(jnp.float32)
    return high, x - high


def sublane(shape):
    return lax.broadcasted_iota(jnp.int32, shape, 0)


def halo(positions, stiff_v):
    count = lax.axis_size(AXES)
    tail = jnp.concatenate([positions[:, -2], positions[:, -1], stiff_v[-1:]], axis=0)
    head = jnp.concatenate([positions[:, 0], positions[:, 1]], axis=0)
    above = lax.ppermute(tail, AXES, [(i, (i + 1) % count) for i in range(count)])
    below = lax.ppermute(head, AXES, [((i + 1) % count, i) for i in range(count)])
    return above, below


def around(x, rows, cols):
    if rows:
        return pltpu.roll(x, rows % x.shape[0], 0)
    return pltpu.roll(x, cols % x.shape[1], 1)


def surface_laplacian(x):
    return around(x, -1, 0) + around(x, 1, 0) + around(x, 0, 1) + around(x, 0, -1) - 4.0 * x


def membrane_force(positions_ref, above_ref, below_ref, stiff_h_ref, stiff_v_ref, wide_ref, force_ref):
    rows = stiff_h_ref.shape[0]
    inner = slice(8, 8 + rows)
    stiff_h = stiff_h_ref[...]
    stiff_v = stiff_v_ref[...]
    wide_ref[3, inner, :] = stiff_v
    wide_ref[3, 7:8, :] = above_ref[6:7]
    stiff_before = wide_ref[3, 7 : 7 + rows, :]
    for k in range(3):
        wide_ref[k, inner, :] = positions_ref[k]
        wide_ref[k, 6:7, :] = above_ref[k : k + 1]
        wide_ref[k, 7:8, :] = above_ref[3 + k : 4 + k]
        wide_ref[k, 8 + rows : 9 + rows, :] = below_ref[k : k + 1]
        wide_ref[k, 9 + rows : 10 + rows, :] = below_ref[3 + k : 4 + k]
        wide = wide_ref[k]
        middle = wide[inner]
        pulling = (
            stiff_h * (around(middle, 0, -1) - middle)
            + around(stiff_h, 0, 1) * (around(middle, 0, 1) - middle)
            + stiff_v * (around(wide, -1, 0)[inner] - middle)
            + stiff_before * (around(wide, 1, 0)[inner] - middle)
        )
        bending = surface_laplacian(surface_laplacian(wide))[inner]
        force_ref[k] = pulling - bend_modulus * bending


def one_hot(count, centred):
    shape = (count, centred.shape[1])
    row = (sublane(shape) - count // 2).astype(jnp.bfloat16)
    return jnp.where(row == centred, jnp.bfloat16(1), jnp.bfloat16(0))


def fetch(pairs, sems):
    copies = [pltpu.make_async_copy(far, here, sems.at[i]) for i, (far, here) in enumerate(pairs)]
    for copy in copies:
        copy.start()
    for copy in copies:
        copy.wait()


def rank_kernel(owner_far, rank_ref, owner_ref, base_ref, sems):
    fetch([(owner_far, owner_ref)], sems)
    owners = base_ref.shape[0]
    row = lax.broadcasted_iota(jnp.int32, (LANES, LANES), 0)
    col = lax.broadcasted_iota(jnp.int32, (LANES, LANES), 1)
    before = jnp.where(row < col, 1.0, 0.0).astype(jnp.bfloat16)
    base_ref[...] = jnp.zeros_like(base_ref)

    def ranks(r, carry):
        at = pl.ds(pl.multiple_of(r * LANES, LANES), LANES)
        own = owner_ref[:, at]
        hot = jnp.where(sublane((owners, LANES)) == own, 1.0, 0.0)
        earlier = dot(hot.astype(jnp.bfloat16), before, NN) + base_ref[...]
        rank_ref[:, at] = jnp.sum(hot * earlier, axis=0, keepdims=True)
        base_ref[...] = base_ref[...] + jnp.sum(hot, axis=1, keepdims=True)
        return carry

    lax.fori_loop(0, owner_ref.shape[1] // LANES, ranks, 0, unroll=8)


def pack_kernel(
    rank_far,
    owner_far,
    element_far,
    coords_far,
    positions_far,
    stiff_h_far,
    stiff_v_far,
    above_ref,
    below_ref,
    out_ref,
    rank_ref,
    owner_ref,
    element_ref,
    coords_ref,
    positions_ref,
    stiff_h_ref,
    stiff_v_ref,
    wide_ref,
    force_ref,
    acc_ref,
    sems,
    *,
    capacity,
):
    fetch(
        [
            (rank_far, rank_ref),
            (owner_far, owner_ref),
            (element_far, element_ref),
            (coords_far, coords_ref),
            (positions_far, positions_ref),
            (stiff_h_far, stiff_h_ref),
            (stiff_v_far, stiff_v_ref),
        ],
        sems,
    )
    units, _, unit = out_ref.shape
    width = acc_ref.shape[1]
    blocks = units * unit // width
    markers = owner_ref.shape[1]
    columns = force_ref.shape[2]
    lines = 4
    step = lines * columns
    membrane_force(positions_ref, above_ref, below_ref, stiff_h_ref, stiff_v_ref, wide_ref, force_ref)
    acc_ref[...] = jnp.zeros_like(acc_ref)

    def route(r, carry):
        at = pl.ds(pl.multiple_of(r * step, step), step)
        slot = owner_ref[:, at].astype(jnp.float32) * float(capacity) + rank_ref[:, at]
        block = jnp.floor((slot + 0.5) * (1.0 / width))
        inside = (slot - block * width - width // 2).astype(jnp.bfloat16)
        block = jnp.broadcast_to(block, (16, step)).astype(jnp.bfloat16)
        force = [
            jnp.concatenate([force_ref[k, pl.ds(lines * r + i, 1), :] for i in range(lines)], axis=1)
            for k in range(3)
        ]
        payload = jnp.concatenate(
            [
                coords_ref[:, at],
                *force,
                element_ref[:, at].astype(jnp.float32) + 1.0,
                jnp.zeros((1, step), jnp.float32),
            ],
            axis=0,
        )
        both = jnp.concatenate(split(payload), axis=0).astype(jnp.bfloat16)
        left = jnp.concatenate(
            [jnp.where(block == jnp.bfloat16(h), both, jnp.bfloat16(0)) for h in range(blocks)], axis=0
        )
        acc_ref[...] += dot(left, one_hot(width, inside), NT)
        return carry

    lax.fori_loop(0, markers // step, route, 0)
    for u in range(units):
        h, at = u * unit // width, u * unit % width
        out_ref[u] = acc_ref[16 * h : 16 * h + 8, at : at + unit] + acc_ref[16 * h + 8 : 16 * h + 16, at : at + unit]


def block_of(got_ref, i, per, capacity):
    count = per * capacity // got_ref.shape[2]
    return jnp.concatenate([got_ref[i * count + j] for j in range(count)], axis=1)


def find_places(got_ref, place_ref, range_ref, hot_ref):
    sources, capacity = place_ref.shape
    groups = range_ref.shape[0]
    row = lax.broadcasted_iota(jnp.int32, (capacity, capacity), 0)
    col = lax.broadcasted_iota(jnp.int32, (capacity, capacity), 1)
    before = jnp.where(row < col, 1.0, 0.0).astype(jnp.bfloat16)
    kind = sublane((groups, capacity)).astype(jnp.float32)
    for s in range(sources):
        group = jnp.floor((block_of(got_ref, s, 1, capacity)[6:7] - 1.0) * (1.0 / GROUP))
        hot_ref[s * groups : (s + 1) * groups, :] = jnp.where(kind == group, 1.0, 0.0)
    earlier = dot(hot_ref[...].astype(jnp.bfloat16), before, NN)
    count = jnp.sum(hot_ref[...], axis=1, keepdims=True)
    total = jnp.zeros((groups, 1), jnp.float32)
    for s in range(sources):
        total = total + count[s * groups : (s + 1) * groups]
    total = jnp.floor((total + (LANES - 1)) * (1.0 / LANES)) * LANES
    start = jnp.zeros((groups, 1), jnp.float32)
    for g in range(groups):
        start = start + jnp.where(sublane((groups, 1)) > g, total[g : g + 1], 0.0)
    base = start + 1.0
    for s in range(sources):
        rows = slice(s * groups, (s + 1) * groups)
        spot = jnp.sum(hot_ref[rows, :] * (earlier[rows] + base), axis=0, keepdims=True) - 1.0
        place_ref[s : s + 1, :] = spot
        base = base + count[rows]
    edge = (lax.broadcasted_iota(jnp.int32, range_ref.shape, 1) * LANES).astype(jnp.float32)
    group = jnp.sum(jnp.where(start + total <= edge, 1.0, 0.0), axis=0, keepdims=True)
    group = jnp.minimum(group, groups - 1.0)
    used = jnp.sum(total, axis=0, keepdims=True) * (1.0 / LANES) + jnp.zeros_like(group)
    range_ref[...] = jnp.where(sublane(range_ref.shape) == 0, group, used).astype(jnp.int32)


def spots(place_ref, i, per):
    spot = jnp.concatenate([place_ref[pl.ds(i * per + j, 1), :] for j in range(per)], axis=1)
    high = jnp.floor(spot * (1.0 / LANES))
    return high, (spot - high * LANES - LANES // 2).astype(jnp.bfloat16)


def batch_of(sources, capacity):
    per = 1
    while per < sources and (per * capacity) % 512 != 0:
        per *= 2
    return per


def sort_markers(got_ref, place_ref, out_ref, acc_ref):
    sources, capacity = place_ref.shape
    chunks = out_ref.shape[0]
    per = batch_of(sources, capacity)
    acc_ref[...] = jnp.zeros_like(acc_ref)

    def gather(i, carry):
        payload = block_of(got_ref, i, per, capacity)
        both = jnp.concatenate(split(payload), axis=0).astype(jnp.bfloat16)
        high, low = spots(place_ref, i, per)
        high = jnp.broadcast_to(high, (16, per * capacity)).astype(jnp.bfloat16)
        left = jnp.concatenate(
            [jnp.where(high == jnp.bfloat16(h), both, jnp.bfloat16(0)) for h in range(chunks)], axis=0
        )
        acc_ref[...] += dot(left, one_hot(LANES, low), NT)
        return carry

    lax.fori_loop(0, sources // per, gather, 0)
    for h in range(chunks):
        out_ref[h] = acc_ref[16 * h : 16 * h + 8] + acc_ref[16 * h + 8 : 16 * h + 16]


def return_samples(place_ref, sampled_ref, out_ref):
    sources, _, capacity = out_ref.shape
    chunks = sampled_ref.shape[0] // 8
    per = batch_of(sources, capacity)
    table = sampled_ref[...].astype(jnp.bfloat16)

    def scatter(i, carry):
        high, low = spots(place_ref, i, per)
        high = jnp.broadcast_to(high, (8, per * capacity))
        picked = dot(table, one_hot(LANES, low), NN)
        total = jnp.zeros((8, per * capacity), jnp.float32)
        for h in range(chunks):
            total = jnp.where(high == float(h), picked[8 * h : 8 * h + 8], total)
        total = total[0:4] + total[4:8]
        for j in range(per):
            out_ref[i * per + j] = total[:, j * capacity : (j + 1) * capacity]
        return carry

    lax.fori_loop(0, sources // per, scatter, 0)


def basis_rows(x):
    node = sublane((POINTS, x.shape[1]))
    value = jnp.zeros((POINTS, x.shape[1]), jnp.float32)
    for i in range(POINTS):
        value = jnp.where(node == i, float(SCALE[i]), value)
    for j in range(POINTS):
        value = value * jnp.where(node == j, 1.0, x - float(ABSCISSA[j]))
    return value


def build_weights(payload, weight_ref):
    along_r = basis_rows(payload[0:1])
    along_s = basis_rows(payload[1:2])
    along_t = basis_rows(payload[2:3])
    step = POINTS * POINTS
    for lane in range(0, LANES, 128):
        at = slice(lane, lane + 128)
        t = along_t[:, at]
        plane = jnp.concatenate([along_s[b : b + 1, at] * t for b in range(POINTS)], axis=0)
        for a in range(POINTS):
            block = along_r[a : a + 1, at] * plane
            high = block.astype(jnp.bfloat16)
            weight_ref[0, a * step : (a + 1) * step, at] = high
            weight_ref[1, a * step : (a + 1) * step, at] = (block - high.astype(jnp.float32)).astype(jnp.bfloat16)


def prepare_kernel(velocity_ref, out_ref):
    groups = out_ref.shape[0]
    for g in range(groups):
        for k in range(3):
            high, low = split(velocity_ref[k, g * GROUP : (g + 1) * GROUP, :])
            out_ref[g, k * GROUP : (k + 1) * GROUP, :] = high.astype(jnp.bfloat16)
            out_ref[g, (3 + k) * GROUP : (4 + k) * GROUP, :] = low.astype(jnp.bfloat16)


def hot_elements(payload, g):
    return jnp.where(
        sublane((GROUP, LANES)).astype(jnp.float32) + (g * GROUP + 1).astype(jnp.float32) == payload[6:7], 1.0, 0.0
    )


def pipeline(range_ref, visit, sorted_ref, weight_refs):
    depth = len(weight_refs)
    last = sorted_ref.shape[0] - 1
    for j in range(depth):
        build_weights(sorted_ref[j], weight_refs[j])

    def several(i, carry):
        for j in range(depth):
            c = depth * i + j
            visit(c, range_ref[0, c], weight_refs[j])
            build_weights(sorted_ref[jnp.minimum(c + depth, last)], weight_refs[j])
        return carry

    lax.fori_loop(0, (range_ref[1, 0] + (depth - 1)) // depth, several, 0)


def interpolate_kernel(
    got_ref,
    velocity_ref,
    out_ref,
    sorted_ref,
    range_ref,
    place_ref,
    hot_ref,
    acc_ref,
    sampled_ref,
    scalar_ref,
    sem_ref,
    *weight_refs,
):
    find_places(got_ref, place_ref, range_ref, hot_ref)
    spans = pltpu.make_async_copy(range_ref, scalar_ref, sem_ref)
    spans.start()
    sort_markers(got_ref, place_ref, sorted_ref, acc_ref)
    spans.wait()
    sampled_ref[...] = jnp.zeros_like(sampled_ref)

    def visit(c, g, weight_ref):
        wide = dot(velocity_ref[g], weight_ref[0], NN)
        narrow = dot(velocity_ref[g, 0 : 3 * GROUP], weight_ref[1], NN)
        total = wide[: 3 * GROUP] + wide[3 * GROUP :] + narrow
        hot = hot_elements(sorted_ref[c], g)
        sums = [jnp.sum(hot * total[k * GROUP : (k + 1) * GROUP], axis=0, keepdims=True) for k in range(3)]
        parts = split(jnp.concatenate(sums + [jnp.zeros((1, LANES), jnp.float32)], axis=0))
        sampled_ref[pl.ds(pl.multiple_of(c * 8, 8), 8), :] = jnp.concatenate(parts, axis=0)

    pipeline(scalar_ref, visit, sorted_ref, weight_refs)
    return_samples(place_ref, sampled_ref, out_ref)


def deposit_kernel(range_ref, sorted_ref, out_ref, *weight_refs):
    out_ref[...] = jnp.zeros_like(out_ref)

    def visit(c, g, weight_ref):
        payload = sorted_ref[c]
        hot = hot_elements(payload, g)
        left = jnp.concatenate(
            [hot * part[3 + k : 4 + k] for part in split(payload) for k in range(3)], axis=0
        ).astype(jnp.bfloat16)
        wide = dot(left, weight_ref[0], NT)
        narrow = dot(left[: 3 * GROUP], weight_ref[1], NT)
        total = wide[: 3 * GROUP] + wide[3 * GROUP :] + narrow
        rows = pl.ds(pl.multiple_of(g * GROUP, GROUP), GROUP)
        for k in range(3):
            out_ref[k, rows, :] += total[k * GROUP : (k + 1) * GROUP]

    pipeline(range_ref, visit, sorted_ref, weight_refs)


def unpack_kernel(owner_ref, rank_ref, arrived_ref, positions_ref, out_ref):
    owners, _, capacity = arrived_ref.shape
    columns = positions_ref.shape[2]
    lines = 4
    step = lines * columns
    rows = []
    for d in range(owners):
        rows.extend(split(arrived_ref[d]))
    table = jnp.concatenate(rows, axis=0).astype(jnp.bfloat16)

    def chunk(r, carry):
        at = pl.ds(pl.multiple_of(r * step, step), step)
        own = jnp.broadcast_to(owner_ref[:, at], (8, step))
        rank = (rank_ref[:, at] - capacity // 2).astype(jnp.bfloat16)
        picked = dot(table, one_hot(capacity, rank), NN)
        total = jnp.zeros((8, step), jnp.float32)
        for d in range(owners):
            total = jnp.where(own == d, picked[8 * d : 8 * d + 8], total)
        moved = total[0:4] + total[4:8]
        for k in range(3):
            for i in range(lines):
                row = pl.ds(lines * r + i, 1)
                part = moved[k : k + 1, i * columns : (i + 1) * columns]
                out_ref[k, row, :] = positions_ref[k, row, :] + time_step * part
        return carry

    lax.fori_loop(0, owner_ref.shape[1] // step, chunk, 0)


def near(*arrays):
    return [pltpu.with_memory_space_constraint(x, pltpu.VMEM) for x in arrays]


def away(*arrays):
    return [pltpu.with_memory_space_constraint(x, pltpu.HBM) for x in arrays]


def exchange(x):
    return lax.all_to_all(x, AXES, 0, 0, tiled=True)


def local(velocity, positions, stiff_h, stiff_v, marker_owner, marker_element, marker_coords):
    devices = lax.axis_size(AXES)
    markers = marker_owner.shape[0]
    capacity = 3 * markers // (2 * devices)
    slots = devices * capacity
    elements = velocity.shape[1]
    groups = elements // GROUP
    f32 = jnp.float32

    above, below = halo(positions, stiff_v)
    owner = marker_owner.reshape(1, markers)
    element = marker_element.reshape(1, markers)
    hbm = pl.BlockSpec(memory_space=pltpu.HBM)
    vector = pl.BlockSpec(memory_space=pltpu.VMEM)
    rank = pl.pallas_call(
        rank_kernel,
        out_shape=jax.ShapeDtypeStruct((1, markers), f32),
        in_specs=[hbm],
        scratch_shapes=[
            pltpu.VMEM((1, markers), jnp.int32),
            pltpu.VMEM((devices, 1), f32),
            pltpu.SemaphoreType.DMA((1,)),
        ],
        compiler_params=SMALL,
        name="rank",
    )(*away(owner))
    rows, columns = stiff_h.shape
    whole = capacity % 128 == 0 and slots % LANES == 0
    unit = 128 if whole else capacity
    width = LANES if whole else capacity
    far = (rank, owner, element, marker_coords, positions, stiff_h, stiff_v)
    outgoing = pl.pallas_call(
        functools.partial(pack_kernel, capacity=capacity),
        out_shape=jax.ShapeDtypeStruct((slots // unit, 8, unit), f32),
        in_specs=[hbm] * 7 + [vector] * 2,
        scratch_shapes=[
            *[pltpu.VMEM(x.shape, x.dtype) for x in far],
            pltpu.VMEM((4, rows + 16, columns), f32),
            pltpu.VMEM((3, rows, columns), f32),
            pltpu.VMEM((slots // width * 16, width), f32),
            pltpu.SemaphoreType.DMA((7,)),
        ],
        compiler_params=SMALL,
        name="pack",
    )(*away(*far), *near(above, below))
    got = exchange(outgoing)
    table = pl.pallas_call(
        prepare_kernel,
        out_shape=pltpu.VMEM((groups, 6 * GROUP, NODES), jnp.bfloat16),
        compiler_params=SMALL,
        name="prepare",
    )(*near(velocity))
    chunks = slots // LANES + groups
    weights = pltpu.VMEM((2, NODES, LANES), jnp.bfloat16)
    returning, ordered, spans = pl.pallas_call(
        interpolate_kernel,
        out_shape=(
            pltpu.VMEM((devices, 4, capacity), f32),
            pltpu.VMEM((chunks, 8, LANES), f32),
            jax.ShapeDtypeStruct((groups, 128), jnp.int32),
        ),
        scratch_shapes=[
            pltpu.VMEM((devices, capacity), f32),
            pltpu.VMEM((devices * groups, capacity), f32),
            pltpu.VMEM((chunks * 16, LANES), f32),
            pltpu.VMEM((chunks * 8, LANES), f32),
            pltpu.SMEM((groups, 128), jnp.int32),
            pltpu.SemaphoreType.DMA,
            *[weights] * DEPTH,
        ],
        compiler_params=SMALL,
        name="interpolate",
    )(*near(got, table))
    arrived = exchange(returning)
    node_forces = pl.pallas_call(
        deposit_kernel,
        out_shape=jax.ShapeDtypeStruct(velocity.shape, f32),
        in_specs=[pl.BlockSpec(memory_space=pltpu.SMEM), pl.BlockSpec(memory_space=pltpu.VMEM)],
        scratch_shapes=[weights] * DEPTH,
        compiler_params=SMALL,
        name="deposit",
    )(spans, *near(ordered))
    moved = pl.pallas_call(
        unpack_kernel,
        out_shape=jax.ShapeDtypeStruct(positions.shape, f32),
        compiler_params=SMALL,
        name="unpack",
    )(*near(owner, rank, arrived, positions))
    return moved, node_forces


def solution(mesh):
    return jax.shard_map(
        local,
        mesh=mesh,
        in_specs=(
            P(None, AXES, None),
            P(None, AXES, None),
            P(AXES, None),
            P(AXES, None),
            P(AXES, None),
            P(AXES),
            P(None, AXES),
        ),
        out_specs=(P(None, AXES, None), P(None, AXES, None)),
        check_vma=False,
    )
```

time: 113 us -> 82.8 us (0.73)
  the two profiles are of different devices: /device:TPU:3 before, /device:TPU:0 now
where the time goes in v2:
time: 82.8 us; the launch traced here: 83.3 us
  Pallas kernels  53.7 us (65%)
  starting transfers between devices  13.5 us (16%)
  waiting for transfers between devices  13 us (16%)
  local copies, waits for them, and re-layouts  2.28 us (3%)
    pallas_call x1, Pallas kernels, local(): pl.pallas_call(interpolate_kernel, out_shape=(pltpu.VMEM((devices, 4, cap...  25.1 us
    pallas_call x1, Pallas kernels, local(): pl.pallas_call(deposit_kernel, out_shape=jax.ShapeDtypeStruct(velocity.sh...  14.7 us
    all_to_all x2, waiting for transfers between devices, exchange(): return lax.all_to_all(x, AXES, 0, 0, tiled=True)  13 us
    pallas_call x1, Pallas kernels, local(): pl.pallas_call(functools.partial(pack_kernel, capacity=capacity), out_sha...  7.19 us
    all_to_all x2, starting transfers between devices, exchange(): return lax.all_to_all(x, AXES, 0, 0, tiled=True)  6.95 us
    ppermute x1, starting transfers between devices, halo(): lax.ppermute(head, AXES, [((i + 1) % count, i) for i in range(count)])  5.99 us
    pallas_call x1, Pallas kernels, local(): pl.pallas_call(unpack_kernel, out_shape=jax.ShapeDtypeStruct(positions.sh...  4.36 us
    pallas_call x1, Pallas kernels, local(): pl.pallas_call(rank_kernel, out_shape=jax.ShapeDtypeStruct((1, markers),...  2.2 us
  transfers between devices with their start and end apart: 4, of which 1 were waited for; matrix products, arithmetic and copies ran while one was open for 0% of the time, Pallas kernels for 21%

profile of v2, /device:TPU:0, one launch (start us, length us, event | category | flops | bytes accessed | tf_op | source)
XLA Modules:
  0.0 83.3 jit_solution(4028812973420639060)
XLA Ops:
  0.6 0.0 copy-start
  0.6 0.8 slice.17
  1.5 0.8 fusion
  2.3 0.5 collective-permute-start
  2.9 6.0 %collective-permute-start.1 = (f32[6,256]{1,0:T(8,128)S(1)}, f32[6,256]{1,0:T(8,128)S(1)}, u32[]{:S(2)}, u32[]{:S(2)}) collective-permute-start(f32[6,256]{1,0:T(8,128)S(1)} %pad_maximum_fusion.1), channel_id=1, source_target_pairs={{1,0},{2,1},{3,2},{4,3},{5,4},{6,5},{7,6},{8,7},{9,8},{10,9},{11,1... | collective-permute-start | bytes 18440 | tf_op jit(solution)/shard_map/ppermute | solution.py:49
  8.9 2.2 %rank.1.rank_far.rank_ref = f32[1,8192]{1,0:T(1,128)S(1)} custom-call(s32[1,8192]{1,0:T(1,128)} %bitcast.10), custom_call_target="tpu_custom_call" | custom-call | tf_op jit(solution)/shard_map/rank/pallas_call | solution.py:460
  11.1 0.0 copy-start.3
  11.1 0.6 copy-done.3
  11.7 0.0 collective-permute-done.1.below_ref
  11.7 0.0 collective-permute-done.above_ref
  11.7 7.2 %pack.1 = f32[96,8,128]{2,1,0:T(8,128)} custom-call(f32[1,8192]{1,0:T(1,128)} %copy-done.3, s32[1,8192]{1,0:T(1,128)} %bitcast.11, s32[1,8192]{1,0:T(1,128)} %bitcast.13, f32[3,8192]{1,0:T(4,128)} %coords_far.1, f32[3,32,256]{2,1,0:T(8,128)} %positions_ref.1, f32[32,256]{1,0:T(8,128)} %stiff_h_far.1, f32[32,256]{1,0:T(8,128)} %stiff_v_far.1, ...), custom_call_target="tpu_custom_call" | custom-call | tf_op jit(solution)/shard_map/pack/pallas_call | solution.py:477
  18.9 4.2 %all-to-all-start = ((f32[96,8,128]{2,1,0:T(8,128)}), f32[96,8,128]{2,1,0:T(8,128)S(1)}, u32[]{:S(2)}, u32[]{:S(2)}) async-start(f32[96,8,128]{2,1,0:T(8,128)} %pack.1), calls=%async_computation | async-start | bytes 786432 | tf_op jit(solution)/shard_map/all_to_all | solution.py:443
  23.1 0.0 copy-done
  23.1 0.2 prepare.1.velocity_ref
  23.3 13.0 %all-to-all-done.got_ref = f32[96,8,128]{2,1,0:T(8,128)S(1)} async-done(((f32[96,8,128]{2,1,0:T(8,128)}), f32[96,8,128]{2,1,0:T(8,128)S(1)}, u32[]{:S(2)}, u32[]{:S(2)}) %all-to-all-start) | async-done | bytes 393248 | tf_op jit(solution)/shard_map/all_to_all | solution.py:443
  36.4 25.1 %interpolate.1 = (f32[32,4,384]{2,1,0:T(4,128)}, f32[56,8,256]{2,1,0:T(8,128)S(1)}, s32[8,128]{1,0:T(8,128)S(1)}) custom-call(f32[96,8,128]{2,1,0:T(8,128)S(1)} %all-to-all-done.got_ref, bf16[8,192,512]{2,1,0:T(8,128)(2,1)S(1)} %prepare.1.velocity_ref), custom_call_target="tpu_custom_call" | custom-call | tf_op jit(solution)/shard_map/interpolate/pallas_call | solution.py:500
  61.5 0.0 copy-start.1
  61.5 0.0 copy-start.2
  61.5 0.0 copy-start.4
  61.5 2.7 %all-to-all-start.1 = ((f32[32,4,384]{2,1,0:T(4,128)}), f32[32,4,384]{2,1,0:T(4,128)S(1)}, u32[]{:S(2)}, u32[]{:S(2)}) async-start(f32[32,4,384]{2,1,0:T(4,128)} %get-tuple-element.5), calls=%async_computation.1 | async-start | bytes 393216 | tf_op jit(solution)/shard_map/all_to_all | solution.py:443
  64.2 14.7 %deposit.1 = f32[3,256,512]{2,1,0:T(8,128)} custom-call(s32[8,128]{1,0:T(8,128)S(1)} %get-tuple-element.6.range_ref, f32[56,8,256]{2,1,0:T(8,128)S(1)} %get-tuple-element.7.sorted_ref), custom_call_target="tpu_custom_call" | custom-call | tf_op jit(solution)/shard_map/deposit/pallas_call | solution.py:520
  78.9 0.0 all-to-all-done.1.arrived_ref
  78.9 0.0 copy-done.1
  78.9 0.0 copy-done.2
  78.9 0.0 copy-done.4
  79.0 4.4 %unpack.1 = f32[3,32,256]{2,1,0:T(8,128)} custom-call(s32[1,8192]{1,0:T(1,128)S(1)} %bitcast.12, f32[1,8192]{1,0:T(1,128)S(1)} %copy-done.4, f32[32,4,384]{2,1,0:T(4,128)S(1)} %all-to-all-done.1.arrived_ref, f32[3,32,256]{2,1,0:T(8,128)S(1)} %copy-done.1), custom_call_target="tpu_custom_call" | custom-call | tf_op jit(solution)/shard_map/unpack/pallas_call | solution.py:528
  (4 shorter events, 0.0 us)
Async XLA Ops:
  0.6 22.5 %copy-start = (f32[3,256,512]{2,1,0:T(8,128)S(1)}, f32[3,256,512]{2,1,0:T(8,128)}, u32[]{:S(2)}) copy-start(f32[3,256,512]{2,1,0:T(8,128)} %velocity_ref.1) | copy-start | bytes 4718596
  2.3 9.4 %collective-permute-start = (f32[7,256]{1,0:T(8,128)S(1)}, f32[7,256]{1,0:T(8,128)S(1)}, u32[]{:S(2)}, u32[]{:S(2)}) collective-permute-start(f32[7,256]{1,0:T(8,128)S(1)} %pad_maximum_fusion), channel_id=1, source_target_pairs={{0,1},{1,2},{2,3},{3,4},{4,5},{5,6},{6,7},{7,8},{8,9},{9,10},{10,1... | collective-permute-start | bytes 21512 | tf_op jit(solution)/shard_map/ppermute | solution.py:48
  2.9 8.8 %collective-permute-start.1 = (f32[6,256]{1,0:T(8,128)S(1)}, f32[6,256]{1,0:T(8,128)S(1)}, u32[]{:S(2)}, u32[]{:S(2)}) collective-permute-start(f32[6,256]{1,0:T(8,128)S(1)} %pad_maximum_fusion.1), channel_id=1, source_target_pairs={{1,0},{2,1},{3,2},{4,3},{5,4},{6,5},{7,6},{8,7},{9,8},{10,9},{11,1... | collective-permute-start | bytes 18440 | tf_op jit(solution)/shard_map/ppermute | solution.py:49
  11.1 0.6 copy-start.3
  18.9 17.5 %all-to-all-start = ((f32[96,8,128]{2,1,0:T(8,128)}), f32[96,8,128]{2,1,0:T(8,128)S(1)}, u32[]{:S(2)}, u32[]{:S(2)}) async-start(f32[96,8,128]{2,1,0:T(8,128)} %pack.1), calls=%async_computation | async-start | bytes 786432 | tf_op jit(solution)/shard_map/all_to_all | solution.py:443
  61.5 17.5 %copy-start.1 = (f32[3,32,256]{2,1,0:T(8,128)S(1)}, f32[3,32,256]{2,1,0:T(8,128)}, u32[]{:S(2)}) copy-start(f32[3,32,256]{2,1,0:T(8,128)} %positions_ref.1) | copy-start | bytes 294916
  61.5 17.5 %copy-start.2 = (s32[8192,1]{0,1:T(1,128)S(1)}, s32[8192,1]{0,1:T(1,128)}, u32[]{:S(2)}) copy-start(s32[8192,1]{0,1:T(1,128)} %param.11) | copy-start | bytes 98308
  61.5 17.5 %copy-start.4 = (f32[1,8192]{1,0:T(1,128)S(1)}, f32[1,8192]{1,0:T(1,128)}, u32[]{:S(2)}) copy-start(f32[1,8192]{1,0:T(1,128)} %copy-done.3) | copy-start | bytes 98308
  61.5 17.4 %all-to-all-start.1 = ((f32[32,4,384]{2,1,0:T(4,128)}), f32[32,4,384]{2,1,0:T(4,128)S(1)}, u32[]{:S(2)}, u32[]{:S(2)}) async-start(f32[32,4,384]{2,1,0:T(4,128)} %get-tuple-element.5), calls=%async_computation.1 | async-start | bytes 393216 | tf_op jit(solution)/shard_map/all_to_all | solution.py:443

commit v3 on v2

--- a/solution.py
+++ b/solution.py
@@ -9,7 +9,6 @@
 from jax.sharding import PartitionSpec as P
 
 POINTS = 8
-NODES = POINTS * POINTS * POINTS
 AXES = ("gx", "gy")
 SMALL = pltpu.CompilerParams(vmem_limit_bytes=20 * 1024 * 1024)
 LANES = 256
@@ -43,8 +42,9 @@
 
 def halo(positions, stiff_v):
     count = lax.axis_size(AXES)
-    tail = jnp.concatenate([positions[:, -2], positions[:, -1], stiff_v[-1:]], axis=0)
-    head = jnp.concatenate([positions[:, 0], positions[:, 1]], axis=0)
+    stacked = jnp.concatenate([positions, stiff_v[None]], axis=0)
+    tail = stacked[:, -2:]
+    head = stacked[:, :2]
     above = lax.ppermute(tail, AXES, [(i, (i + 1) % count) for i in range(count)])
     below = lax.ppermute(head, AXES, [((i + 1) % count, i) for i in range(count)])
     return above, below
@@ -66,14 +66,12 @@
     stiff_h = stiff_h_ref[...]
     stiff_v = stiff_v_ref[...]
     wide_ref[3, inner, :] = stiff_v
-    wide_ref[3, 7:8, :] = above_ref[6:7]
+    wide_ref[3, 7:8, :] = above_ref[3, 1:2, :]
     stiff_before = wide_ref[3, 7 : 7 + rows, :]
     for k in range(3):
         wide_ref[k, inner, :] = positions_ref[k]
-        wide_ref[k, 6:7, :] = above_ref[k : k + 1]
-        wide_ref[k, 7:8, :] = above_ref[3 + k : 4 + k]
-        wide_ref[k, 8 + rows : 9 + rows, :] = below_ref[k : k + 1]
-        wide_ref[k, 9 + rows : 10 + rows, :] = below_ref[3 + k : 4 + k]
+        wide_ref[k, 6:8, :] = above_ref[k]
+        wide_ref[k, 8 + rows : 10 + rows, :] = below_ref[k]
         wide = wide_ref[k]
         middle = wide[inner]
         pulling = (
@@ -92,16 +90,50 @@
     return jnp.where(row == centred, jnp.bfloat16(1), jnp.bfloat16(0))
 
 
-def fetch(pairs, sems):
-    copies = [pltpu.make_async_copy(far, here, sems.at[i]) for i, (far, here) in enumerate(pairs)]
+def spread(payload, label, count):
+    wide = jnp.broadcast_to(label, (16, label.shape[1]))
+    wide = (wide - (sublane(wide.shape) // 8).astype(jnp.float32)).astype(jnp.bfloat16)
+    masks = [wide == jnp.bfloat16(2 * i) for i in range(count // 2)]
+    sides = []
+    for part in split(payload):
+        twice = jnp.concatenate([part, part], axis=0).astype(jnp.bfloat16)
+        sides.append(jnp.concatenate([jnp.where(mask, twice, jnp.bfloat16(0)) for mask in masks], axis=0))
+    return jnp.concatenate(sides, axis=0)
+
+
+def fold(x):
+    half = x.shape[0] // 2
+    return x[:half] + x[half:]
+
+
+def pick(rows, label, right):
+    parts = [part.astype(jnp.bfloat16) for part in split(rows)]
+    if rows.shape[1] % 128 == 0:
+        found = dot(jnp.concatenate(parts, axis=1), jnp.concatenate([right, right], axis=0), NN)
+    else:
+        found = dot(parts[0], right, NN) + dot(parts[1], right, NN)
+    wide = jnp.broadcast_to(label, (8, label.shape[1]))
+    wide = wide - (sublane(wide.shape) // 4).astype(jnp.float32)
+    total = jnp.zeros(wide.shape, jnp.float32)
+    for i in range(rows.shape[0] // 8):
+        total = jnp.where(wide == float(2 * i), found[8 * i : 8 * i + 8], total)
+    return total[0:4] + total[4:8]
+
+
+def stacked_rows(ref):
+    return jnp.concatenate([ref[i] for i in range(ref.shape[0])], axis=0)
+
+
+def rank_kernel(*refs):
+    *refs, base_ref, sems = refs
+    count = (len(refs) - 1) // 2
+    far, near, rank_ref = refs[:count], refs[count : 2 * count], refs[-1]
+    copies = [pltpu.make_async_copy(far[i], near[i], sems.at[i]) for i in range(count)]
     for copy in copies:
         copy.start()
     for copy in copies:
         copy.wait()
-
-
-def rank_kernel(owner_far, rank_ref, owner_ref, base_ref, sems):
-    fetch([(owner_far, owner_ref)], sems)
+    owner_ref = near[0]
     owners = base_ref.shape[0]
     row = lax.broadcasted_iota(jnp.int32, (LANES, LANES), 0)
     col = lax.broadcasted_iota(jnp.int32, (LANES, LANES), 1)
@@ -121,42 +153,24 @@
 
 
 def pack_kernel(
-    rank_far,
-    owner_far,
-    element_far,
-    coords_far,
-    positions_far,
-    stiff_h_far,
-    stiff_v_far,
-    above_ref,
-    below_ref,
-    out_ref,
-    rank_ref,
     owner_ref,
     element_ref,
     coords_ref,
     positions_ref,
     stiff_h_ref,
     stiff_v_ref,
+    rank_ref,
+    above_ref,
+    below_ref,
+    out_ref,
+    kept_ref,
     wide_ref,
     force_ref,
     acc_ref,
-    sems,
     *,
     capacity,
 ):
-    fetch(
-        [
-            (rank_far, rank_ref),
-            (owner_far, owner_ref),
-            (element_far, element_ref),
-            (coords_far, coords_ref),
-            (positions_far, positions_ref),
-            (stiff_h_far, stiff_h_ref),
-            (stiff_v_far, stiff_v_ref),
-        ],
-        sems,
-    )
+    kept_ref[...] = rank_ref[...]
     units, _, unit = out_ref.shape
     width = acc_ref.shape[1]
     blocks = units * unit // width
@@ -172,7 +186,6 @@
         slot = owner_ref[:, at].astype(jnp.float32) * float(capacity) + rank_ref[:, at]
         block = jnp.floor((slot + 0.5) * (1.0 / width))
         inside = (slot - block * width - width // 2).astype(jnp.bfloat16)
-        block = jnp.broadcast_to(block, (16, step)).astype(jnp.bfloat16)
         force = [
             jnp.concatenate([force_ref[k, pl.ds(lines * r + i, 1), :] for i in range(lines)], axis=1)
             for k in range(3)
@@ -186,17 +199,13 @@
             ],
             axis=0,
         )
-        both = jnp.concatenate(split(payload), axis=0).astype(jnp.bfloat16)
-        left = jnp.concatenate(
-            [jnp.where(block == jnp.bfloat16(h), both, jnp.bfloat16(0)) for h in range(blocks)], axis=0
-        )
-        acc_ref[...] += dot(left, one_hot(width, inside), NT)
+        acc_ref[...] += fold(dot(spread(payload, block, blocks), one_hot(width, inside), NT))
         return carry
 
     lax.fori_loop(0, markers // step, route, 0)
     for u in range(units):
         h, at = u * unit // width, u * unit % width
-        out_ref[u] = acc_ref[16 * h : 16 * h + 8, at : at + unit] + acc_ref[16 * h + 8 : 16 * h + 16, at : at + unit]
+        out_ref[u] = acc_ref[8 * h : 8 * h + 8, at : at + unit]
 
 
 def block_of(got_ref, i, per, capacity):
@@ -257,34 +266,23 @@
 
     def gather(i, carry):
         payload = block_of(got_ref, i, per, capacity)
-        both = jnp.concatenate(split(payload), axis=0).astype(jnp.bfloat16)
         high, low = spots(place_ref, i, per)
-        high = jnp.broadcast_to(high, (16, per * capacity)).astype(jnp.bfloat16)
-        left = jnp.concatenate(
-            [jnp.where(high == jnp.bfloat16(h), both, jnp.bfloat16(0)) for h in range(chunks)], axis=0
-        )
-        acc_ref[...] += dot(left, one_hot(LANES, low), NT)
+        acc_ref[...] += fold(dot(spread(payload, high, chunks), one_hot(LANES, low), NT))
         return carry
 
     lax.fori_loop(0, sources // per, gather, 0)
     for h in range(chunks):
-        out_ref[h] = acc_ref[16 * h : 16 * h + 8] + acc_ref[16 * h + 8 : 16 * h + 16]
+        out_ref[h] = acc_ref[8 * h : 8 * h + 8]
 
 
 def return_samples(place_ref, sampled_ref, out_ref):
     sources, _, capacity = out_ref.shape
-    chunks = sampled_ref.shape[0] // 8
     per = batch_of(sources, capacity)
-    table = sampled_ref[...].astype(jnp.bfloat16)
+    rows = stacked_rows(sampled_ref)
 
     def scatter(i, carry):
         high, low = spots(place_ref, i, per)
-        high = jnp.broadcast_to(high, (8, per * capacity))
-        picked = dot(table, one_hot(LANES, low), NN)
-        total = jnp.zeros((8, per * capacity), jnp.float32)
-        for h in range(chunks):
-            total = jnp.where(high == float(h), picked[8 * h : 8 * h + 8], total)
-        total = total[0:4] + total[4:8]
+        total = pick(rows, high, one_hot(LANES, low))
         for j in range(per):
             out_ref[i * per + j] = total[:, j * capacity : (j + 1) * capacity]
         return carry
@@ -302,48 +300,51 @@
     return value
 
 
-def build_weights(payload, weight_ref):
-    along_r = basis_rows(payload[0:1])
+def plane_of(payload):
     along_s = basis_rows(payload[1:2])
     along_t = basis_rows(payload[2:3])
-    step = POINTS * POINTS
-    for lane in range(0, LANES, 128):
-        at = slice(lane, lane + 128)
-        t = along_t[:, at]
-        plane = jnp.concatenate([along_s[b : b + 1, at] * t for b in range(POINTS)], axis=0)
+    return jnp.concatenate([along_s[b : b + 1] * along_t for b in range(POINTS)], axis=0)
+
+
+def build_weights(payload, g, weight_ref):
+    local = payload[6:7] - (g * GROUP + 1 + GROUP // 2).astype(jnp.float32)
+    hot = one_hot(GROUP, local.astype(jnp.bfloat16))
+    for i, part in enumerate(split(basis_rows(payload[0:1]))):
         for a in range(POINTS):
-            block = along_r[a : a + 1, at] * plane
-            high = block.astype(jnp.bfloat16)
-            weight_ref[0, a * step : (a + 1) * step, at] = high
-            weight_ref[1, a * step : (a + 1) * step, at] = (block - high.astype(jnp.float32)).astype(jnp.bfloat16)
+            row = jnp.broadcast_to(part[a : a + 1], (16, LANES)).astype(jnp.bfloat16)
+            weight_ref[i, a * GROUP : (a + 1) * GROUP, :] = hot * jnp.concatenate([row] * (GROUP // 16), axis=0)
 
 
 def prepare_kernel(velocity_ref, out_ref):
     groups = out_ref.shape[0]
+    half = out_ref.shape[1] // 2
+    side = half // 3
     for g in range(groups):
         for k in range(3):
-            high, low = split(velocity_ref[k, g * GROUP : (g + 1) * GROUP, :])
-            out_ref[g, k * GROUP : (k + 1) * GROUP, :] = high.astype(jnp.bfloat16)
-            out_ref[g, (3 + k) * GROUP : (4 + k) * GROUP, :] = low.astype(jnp.bfloat16)
-
-
-def hot_elements(payload, g):
-    return jnp.where(
-        sublane((GROUP, LANES)).astype(jnp.float32) + (g * GROUP + 1).astype(jnp.float32) == payload[6:7], 1.0, 0.0
-    )
+            turned = velocity_ref[k, g * GROUP : (g + 1) * GROUP, :].T
+            tile = jnp.concatenate([turned[a * side : (a + 1) * side] for a in range(POINTS)], axis=1)
+            high, low = split(tile)
+            out_ref[g, k * side : (k + 1) * side, :] = high.astype(jnp.bfloat16)
+            out_ref[g, half + k * side : half + (k + 1) * side, :] = low.astype(jnp.bfloat16)
+
+
+def total_of(wide, narrow):
+    half = narrow.shape[0]
+    return wide[:half] + wide[half:] + narrow
 
 
 def pipeline(range_ref, visit, sorted_ref, weight_refs):
     depth = len(weight_refs)
     last = sorted_ref.shape[0] - 1
     for j in range(depth):
-        build_weights(sorted_ref[j], weight_refs[j])
+        build_weights(sorted_ref[j], range_ref[0, j], weight_refs[j])
 
     def several(i, carry):
         for j in range(depth):
             c = depth * i + j
             visit(c, range_ref[0, c], weight_refs[j])
-            build_weights(sorted_ref[jnp.minimum(c + depth, last)], weight_refs[j])
+            ahead = jnp.minimum(c + depth, last)
+            build_weights(sorted_ref[ahead], range_ref[0, ahead], weight_refs[j])
         return carry
 
     lax.fori_loop(0, (range_ref[1, 0] + (depth - 1)) // depth, several, 0)
@@ -371,56 +372,53 @@
     sampled_ref[...] = jnp.zeros_like(sampled_ref)
 
     def visit(c, g, weight_ref):
+        half = velocity_ref.shape[1] // 2
         wide = dot(velocity_ref[g], weight_ref[0], NN)
-        narrow = dot(velocity_ref[g, 0 : 3 * GROUP], weight_ref[1], NN)
-        total = wide[: 3 * GROUP] + wide[3 * GROUP :] + narrow
-        hot = hot_elements(sorted_ref[c], g)
-        sums = [jnp.sum(hot * total[k * GROUP : (k + 1) * GROUP], axis=0, keepdims=True) for k in range(3)]
-        parts = split(jnp.concatenate(sums + [jnp.zeros((1, LANES), jnp.float32)], axis=0))
-        sampled_ref[pl.ds(pl.multiple_of(c * 8, 8), 8), :] = jnp.concatenate(parts, axis=0)
+        narrow = dot(velocity_ref[g, 0:half], weight_ref[1], NN)
+        total = total_of(wide, narrow)
+        plane = plane_of(sorted_ref[c])
+        side = plane.shape[0]
+        sums = [jnp.sum(plane * total[k * side : (k + 1) * side], axis=0, keepdims=True) for k in range(3)]
+        sampled_ref[c] = jnp.concatenate(sums + [jnp.zeros((1, LANES), jnp.float32)], axis=0)
 
     pipeline(scalar_ref, visit, sorted_ref, weight_refs)
     return_samples(place_ref, sampled_ref, out_ref)
 
 
-def deposit_kernel(range_ref, sorted_ref, out_ref, *weight_refs):
-    out_ref[...] = jnp.zeros_like(out_ref)
+def deposit_kernel(range_ref, sorted_ref, out_ref, sum_ref, *weight_refs):
+    sum_ref[...] = jnp.zeros_like(sum_ref)
 
     def visit(c, g, weight_ref):
         payload = sorted_ref[c]
-        hot = hot_elements(payload, g)
-        left = jnp.concatenate(
-            [hot * part[3 + k : 4 + k] for part in split(payload) for k in range(3)], axis=0
-        ).astype(jnp.bfloat16)
+        plane = plane_of(payload)
+        loads = jnp.concatenate([plane * payload[3 + k : 4 + k] for k in range(3)], axis=0)
+        left = jnp.concatenate([part.astype(jnp.bfloat16) for part in split(loads)], axis=0)
         wide = dot(left, weight_ref[0], NT)
-        narrow = dot(left[: 3 * GROUP], weight_ref[1], NT)
-        total = wide[: 3 * GROUP] + wide[3 * GROUP :] + narrow
-        rows = pl.ds(pl.multiple_of(g * GROUP, GROUP), GROUP)
+        narrow = dot(left[: loads.shape[0]], weight_ref[1], NT)
+        sum_ref[g] += total_of(wide, narrow)
+
+    pipeline(range_ref, visit, sorted_ref, weight_refs)
+    groups, rows, _ = sum_ref.shape
+    side = rows // 3
+    for g in range(groups):
         for k in range(3):
-            out_ref[k, rows, :] += total[k * GROUP : (k + 1) * GROUP]
-
-    pipeline(range_ref, visit, sorted_ref, weight_refs)
+            turned = sum_ref[g, k * side : (k + 1) * side, :].T
+            out_ref[k, g * GROUP : (g + 1) * GROUP, :] = jnp.concatenate(
+                [turned[a * GROUP : (a + 1) * GROUP] for a in range(POINTS)], axis=1
+            )
 
 
 def unpack_kernel(owner_ref, rank_ref, arrived_ref, positions_ref, out_ref):
-    owners, _, capacity = arrived_ref.shape
+    _, _, capacity = arrived_ref.shape
     columns = positions_ref.shape[2]
     lines = 4
     step = lines * columns
-    rows = []
-    for d in range(owners):
-        rows.extend(split(arrived_ref[d]))
-    table = jnp.concatenate(rows, axis=0).astype(jnp.bfloat16)
+    rows = stacked_rows(arrived_ref)
 
     def chunk(r, carry):
         at = pl.ds(pl.multiple_of(r * step, step), step)
-        own = jnp.broadcast_to(owner_ref[:, at], (8, step))
         rank = (rank_ref[:, at] - capacity // 2).astype(jnp.bfloat16)
-        picked = dot(table, one_hot(capacity, rank), NN)
-        total = jnp.zeros((8, step), jnp.float32)
-        for d in range(owners):
-            total = jnp.where(own == d, picked[8 * d : 8 * d + 8], total)
-        moved = total[0:4] + total[4:8]
+        moved = pick(rows, owner_ref[:, at].astype(jnp.float32), one_hot(capacity, rank))
         for k in range(3):
             for i in range(lines):
                 row = pl.ds(lines * r + i, 1)
@@ -450,53 +448,49 @@
     slots = devices * capacity
     elements = velocity.shape[1]
     groups = elements // GROUP
+    side = velocity.shape[2] // POINTS
     f32 = jnp.float32
 
     above, below = halo(positions, stiff_v)
     owner = marker_owner.reshape(1, markers)
     element = marker_element.reshape(1, markers)
     hbm = pl.BlockSpec(memory_space=pltpu.HBM)
-    vector = pl.BlockSpec(memory_space=pltpu.VMEM)
-    rank = pl.pallas_call(
+    far = (owner, element, marker_coords, positions, stiff_h, stiff_v)
+    *close, rank = pl.pallas_call(
         rank_kernel,
-        out_shape=jax.ShapeDtypeStruct((1, markers), f32),
-        in_specs=[hbm],
-        scratch_shapes=[
-            pltpu.VMEM((1, markers), jnp.int32),
-            pltpu.VMEM((devices, 1), f32),
-            pltpu.SemaphoreType.DMA((1,)),
-        ],
+        out_shape=[pltpu.VMEM(x.shape, x.dtype) for x in far] + [pltpu.VMEM((1, markers), f32)],
+        in_specs=[hbm] * len(far),
+        scratch_shapes=[pltpu.VMEM((devices, 1), f32), pltpu.SemaphoreType.DMA((len(far),))],
         compiler_params=SMALL,
         name="rank",
-    )(*away(owner))
+    )(*away(*far))
     rows, columns = stiff_h.shape
     whole = capacity % 128 == 0 and slots % LANES == 0
     unit = 128 if whole else capacity
     width = LANES if whole else capacity
-    far = (rank, owner, element, marker_coords, positions, stiff_h, stiff_v)
-    outgoing = pl.pallas_call(
+    outgoing, kept = pl.pallas_call(
         functools.partial(pack_kernel, capacity=capacity),
-        out_shape=jax.ShapeDtypeStruct((slots // unit, 8, unit), f32),
-        in_specs=[hbm] * 7 + [vector] * 2,
+        out_shape=(
+            jax.ShapeDtypeStruct((slots // unit, 8, unit), f32),
+            jax.ShapeDtypeStruct((1, markers), f32),
+        ),
         scratch_shapes=[
-            *[pltpu.VMEM(x.shape, x.dtype) for x in far],
             pltpu.VMEM((4, rows + 16, columns), f32),
             pltpu.VMEM((3, rows, columns), f32),
-            pltpu.VMEM((slots // width * 16, width), f32),
-            pltpu.SemaphoreType.DMA((7,)),
+            pltpu.VMEM((slots // width * 8, width), f32),
         ],
         compiler_params=SMALL,
         name="pack",
-    )(*away(*far), *near(above, below))
+    )(*near(*close, rank, above, below))
     got = exchange(outgoing)
     table = pl.pallas_call(
         prepare_kernel,
-        out_shape=pltpu.VMEM((groups, 6 * GROUP, NODES), jnp.bfloat16),
+        out_shape=pltpu.VMEM((groups, 6 * side, POINTS * GROUP), jnp.bfloat16),
         compiler_params=SMALL,
         name="prepare",
     )(*near(velocity))
     chunks = slots // LANES + groups
-    weights = pltpu.VMEM((2, NODES, LANES), jnp.bfloat16)
+    weights = pltpu.VMEM((2, POINTS * GROUP, LANES), jnp.bfloat16)
     returning, ordered, spans = pl.pallas_call(
         interpolate_kernel,
         out_shape=(
@@ -507,8 +501,8 @@
         scratch_shapes=[
             pltpu.VMEM((devices, capacity), f32),
             pltpu.VMEM((devices * groups, capacity), f32),
-            pltpu.VMEM((chunks * 16, LANES), f32),
             pltpu.VMEM((chunks * 8, LANES), f32),
+            pltpu.VMEM((chunks, 4, LANES), f32),
             pltpu.SMEM((groups, 128), jnp.int32),
             pltpu.SemaphoreType.DMA,
             *[weights] * DEPTH,
@@ -521,7 +515,7 @@
         deposit_kernel,
         out_shape=jax.ShapeDtypeStruct(velocity.shape, f32),
         in_specs=[pl.BlockSpec(memory_space=pltpu.SMEM), pl.BlockSpec(memory_space=pltpu.VMEM)],
-        scratch_shapes=[weights] * DEPTH,
+        scratch_shapes=[pltpu.VMEM((groups, 3 * side, POINTS * GROUP), f32)] + [weights] * DEPTH,
         compiler_params=SMALL,
         name="deposit",
     )(spans, *near(ordered))
@@ -530,7 +524,7 @@
         out_shape=jax.ShapeDtypeStruct(positions.shape, f32),
         compiler_params=SMALL,
         name="unpack",
-    )(*near(owner, rank, arrived, positions))
+    )(*near(owner, kept, arrived, positions))
     return moved, node_forces
 
 

time: 82.8 us -> 73.9 us (0.89)
  the two profiles are of different devices: /device:TPU:0 before, /device:TPU:1 now
where the time goes in v3:
time: 73.9 us; the launch traced here: 72.9 us
  Pallas kernels  45.4 us (61%)
  starting transfers between devices  13.8 us (19%)
  waiting for transfers between devices  11.4 us (15%)
  other arithmetic  0.91 us (1%)
    pallas_call x1, Pallas kernels, local(): pl.pallas_call(interpolate_kernel, out_shape=(pltpu.VMEM((devices, 4, cap...  19.3 us
    all_to_all x2, starting transfers between devices, exchange(): return lax.all_to_all(x, AXES, 0, 0, tiled=True)  11.1 us
    pallas_call x1, Pallas kernels, local(): pl.pallas_call(deposit_kernel, out_shape=jax.ShapeDtypeStruct(velocity.sh...  10.7 us
    all_to_all x2, waiting for transfers between devices, exchange(): return lax.all_to_all(x, AXES, 0, 0, tiled=True)  9.51 us
    pallas_call x1, Pallas kernels, local(): pl.pallas_call(functools.partial(pack_kernel, capacity=capacity), out_sha...  6.11 us
    pallas_call x1, Pallas kernels, local(): pl.pallas_call(unpack_kernel, out_shape=jax.ShapeDtypeStruct(positions.sh...  3.89 us
    pallas_call x1, Pallas kernels, local(): pl.pallas_call(prepare_kernel, out_shape=pltpu.VMEM((groups, 6 * side, PO...  2.92 us
    ppermute x1, starting transfers between devices, halo(): lax.ppermute(tail, AXES, [(i, (i + 1) % count) for i in range(count)])  2.67 us
  transfers between devices with their start and end apart: 4, of which 2 were waited for; matrix products, arithmetic and copies ran while one was open for 0% of the time, Pallas kernels for 22%

profile of v3, /device:TPU:1, one launch (start us, length us, event | category | flops | bytes accessed | tf_op | source)
XLA Modules:
  0.0 72.9 jit_solution(10550434167177329711)
XLA Ops:
  0.6 0.0 copy-start
  0.6 0.9 %pad_maximum_fusion = (f32[4,2,256]{2,1,0:T(2,128)S(1)}, f32[4,2,256]{2,1,0:T(2,128)S(1)}) fusion(f32[1,32,256]{2,1,0:T(8,128)} %bitcast.5, f32[3,32,256]{2,1,0:T(8,128)} %positions_ref.1), kind=kLoop, calls=%fused_computation | loop fusion | flops 4096 | bytes 147456 | tf_op jit(solution)/shard_map/concatenate | solution.py:45
  1.6 0.1 collective-permute-start.1
  1.6 2.7 %collective-permute-start = (f32[4,2,256]{2,1,0:T(2,128)S(1)}, f32[4,2,256]{2,1,0:T(2,128)S(1)}, u32[]{:S(2)}, u32[]{:S(2)}) collective-permute-start(f32[4,2,256]{2,1,0:T(2,128)S(1)} %get-tuple-element.27), channel_id=1, source_target_pairs={{0,1},{1,2},{2,3},{3,4},{4,5},{5,6},{6,7},{7,8},{8,9},{9,10},{10,1... | collective-permute-start | bytes 24584 | tf_op jit(solution)/shard_map/ppermute | solution.py:48
  4.3 2.5 %rank.1 = (s32[1,8192]{1,0:T(1,128)S(1)}, s32[1,8192]{1,0:T(1,128)S(1)}, f32[3,8192]{1,0:T(4,128)S(1)}, f32[3,32,256]{2,1,0:T(8,128)S(1)}, f32[32,256]{1,0:T(8,1...) custom-call(s32[1,8192]{1,0:T(1,128)} %bitcast.3, s32[1,8192]{1,0:T(1,128)} %bitcast.6, f32[3,8192]{1,0:T(4,128)} %refs_2_.1, ...), custom_call_target="tpu_custom_call" | custom-call | tf_op jit(solution)/shard_map/rank/pallas_call | solution.py:459
  6.8 0.0 collective-permute-done.1.below_ref
  6.8 1.9 %collective-permute-done.above_ref = f32[4,2,256]{2,1,0:T(2,128)S(1)} collective-permute-done((f32[4,2,256]{2,1,0:T(2,128)S(1)}, f32[4,2,256]{2,1,0:T(2,128)S(1)}, u32[]{:S(2)}, u32[]{:S(2)}) %collective-permute-start) | collective-permute-done | bytes 8224 | tf_op jit(solution)/shard_map/ppermute | solution.py:48
  8.7 6.1 %pack.1 = (f32[96,8,128]{2,1,0:T(8,128)}, f32[1,8192]{1,0:T(1,128)S(1)}) custom-call(s32[1,8192]{1,0:T(1,128)S(1)} %get-tuple-element.14.owner_ref, s32[1,8192]{1,0:T(1,128)S(1)} %get-tuple-element.15.element_ref, f32[3,8192]{1,0:T(4,128)S(1)} %get-tuple-element.16.coords_ref, f32[3,32,256]{2,1,0:T(8,128)S(1)} %get-tuple-element.17.positions_ref, ...), custom_call_target="tpu_custom_call" | custom-call | tf_op jit(solution)/shard_map/pack/pallas_call | solution.py:471
  14.8 0.0 copy-start.3
  14.8 0.6 copy-done.3
  15.4 8.2 %all-to-all-start = ((f32[96,8,128]{2,1,0:T(8,128)}), f32[96,8,128]{2,1,0:T(8,128)S(1)}, u32[]{:S(2)}, u32[]{:S(2)}) async-start(f32[96,8,128]{2,1,0:T(8,128)} %get-tuple-element.22), calls=%async_computation | async-start | bytes 786432 | tf_op jit(solution)/shard_map/all_to_all | solution.py:441
  23.6 0.0 copy-done
  23.6 2.9 %prepare.1.velocity_ref = bf16[8,384,256]{2,1,0:T(8,128)(2,1)S(1)} custom-call(f32[3,256,512]{2,1,0:T(8,128)S(1)} %copy-done), custom_call_target="tpu_custom_call" | custom-call | tf_op jit(solution)/shard_map/prepare/pallas_call | solution.py:486
  26.5 9.5 %all-to-all-done.got_ref = f32[96,8,128]{2,1,0:T(8,128)S(1)} async-done(((f32[96,8,128]{2,1,0:T(8,128)}), f32[96,8,128]{2,1,0:T(8,128)S(1)}, u32[]{:S(2)}, u32[]{:S(2)}) %all-to-all-start) | async-done | bytes 393248 | tf_op jit(solution)/shard_map/all_to_all | solution.py:441
  36.0 19.3 %interpolate.1 = (f32[32,4,384]{2,1,0:T(4,128)}, f32[56,8,256]{2,1,0:T(8,128)S(1)}, s32[8,128]{1,0:T(8,128)S(1)}) custom-call(f32[96,8,128]{2,1,0:T(8,128)S(1)} %all-to-all-done.got_ref, bf16[8,384,256]{2,1,0:T(8,128)(2,1)S(1)} %prepare.1.velocity_ref), custom_call_target="tpu_custom_call" | custom-call | tf_op jit(solution)/shard_map/interpolate/pallas_call | solution.py:494
  55.4 0.0 copy-start.1
  55.4 0.0 copy-start.2
  55.4 0.0 copy-start.4
  55.4 2.9 %all-to-all-start.1 = ((f32[32,4,384]{2,1,0:T(4,128)}), f32[32,4,384]{2,1,0:T(4,128)S(1)}, u32[]{:S(2)}, u32[]{:S(2)}) async-start(f32[32,4,384]{2,1,0:T(4,128)} %get-tuple-element.23), calls=%async_computation.1 | async-start | bytes 393216 | tf_op jit(solution)/shard_map/all_to_all | solution.py:441
  58.3 10.7 %deposit.1 = f32[3,256,512]{2,1,0:T(8,128)} custom-call(s32[8,128]{1,0:T(8,128)S(1)} %get-tuple-element.24.range_ref, f32[56,8,256]{2,1,0:T(8,128)S(1)} %get-tuple-element.25.sorted_ref), custom_call_target="tpu_custom_call" | custom-call | tf_op jit(solution)/shard_map/deposit/pallas_call | solution.py:514
  69.0 0.0 all-to-all-done.1.arrived_ref
  69.0 0.0 copy-done.1
  69.0 0.0 copy-done.2
  69.0 0.0 copy-done.4
  69.0 3.9 %unpack.1 = f32[3,32,256]{2,1,0:T(8,128)} custom-call(s32[1,8192]{1,0:T(1,128)S(1)} %bitcast.4, f32[1,8192]{1,0:T(1,128)S(1)} %copy-done.4, f32[32,4,384]{2,1,0:T(4,128)S(1)} %all-to-all-done.1.arrived_ref, f32[3,32,256]{2,1,0:T(8,128)S(1)} %copy-done.1), custom_call_target="tpu_custom_call" | custom-call | tf_op jit(solution)/shard_map/unpack/pallas_call | solution.py:522
Async XLA Ops:
  0.6 23.0 %copy-start = (f32[3,256,512]{2,1,0:T(8,128)S(1)}, f32[3,256,512]{2,1,0:T(8,128)}, u32[]{:S(2)}) copy-start(f32[3,256,512]{2,1,0:T(8,128)} %velocity_ref.1) | copy-start | bytes 4718596
  1.6 5.2 %collective-permute-start.1 = (f32[4,2,256]{2,1,0:T(2,128)S(1)}, f32[4,2,256]{2,1,0:T(2,128)S(1)}, u32[]{:S(2)}, u32[]{:S(2)}) collective-permute-start(f32[4,2,256]{2,1,0:T(2,128)S(1)} %get-tuple-element.26), channel_id=1, source_target_pairs={{1,0},{2,1},{3,2},{4,3},{5,4},{6,5},{7,6},{8,7},{9,8},{10,9},{11,1... | collective-permute-start | bytes 24584 | tf_op jit(solution)/shard_map/ppermute | solution.py:49
  1.6 7.1 %collective-permute-start = (f32[4,2,256]{2,1,0:T(2,128)S(1)}, f32[4,2,256]{2,1,0:T(2,128)S(1)}, u32[]{:S(2)}, u32[]{:S(2)}) collective-permute-start(f32[4,2,256]{2,1,0:T(2,128)S(1)} %get-tuple-element.27), channel_id=1, source_target_pairs={{0,1},{1,2},{2,3},{3,4},{4,5},{5,6},{6,7},{7,8},{8,9},{9,10},{10,1... | collective-permute-start | bytes 24584 | tf_op jit(solution)/shard_map/ppermute | solution.py:48
  14.8 0.6 copy-start.3
  15.4 20.6 %all-to-all-start = ((f32[96,8,128]{2,1,0:T(8,128)}), f32[96,8,128]{2,1,0:T(8,128)S(1)}, u32[]{:S(2)}, u32[]{:S(2)}) async-start(f32[96,8,128]{2,1,0:T(8,128)} %get-tuple-element.22), calls=%async_computation | async-start | bytes 786432 | tf_op jit(solution)/shard_map/all_to_all | solution.py:441
  55.4 13.6 %copy-start.1 = (f32[3,32,256]{2,1,0:T(8,128)S(1)}, f32[3,32,256]{2,1,0:T(8,128)}, u32[]{:S(2)}) copy-start(f32[3,32,256]{2,1,0:T(8,128)} %positions_ref.1) | copy-start | bytes 294916
  55.4 13.6 %copy-start.2 = (s32[8192,1]{0,1:T(1,128)S(1)}, s32[8192,1]{0,1:T(1,128)}, u32[]{:S(2)}) copy-start(s32[8192,1]{0,1:T(1,128)} %param.11) | copy-start | bytes 98308
  55.4 13.6 %copy-start.4 = (f32[1,8192]{1,0:T(1,128)S(1)}, f32[1,8192]{1,0:T(1,128)}, u32[]{:S(2)}) copy-start(f32[1,8192]{1,0:T(1,128)} %copy-done.3) | copy-start | bytes 98308
  55.4 13.6 %all-to-all-start.1 = ((f32[32,4,384]{2,1,0:T(4,128)}), f32[32,4,384]{2,1,0:T(4,128)S(1)}, u32[]{:S(2)}, u32[]{:S(2)}) async-start(f32[32,4,384]{2,1,0:T(4,128)} %get-tuple-element.23), calls=%async_computation.1 | async-start | bytes 393216 | tf_op jit(solution)/shard_map/all_to_all | solution.py:441

commit v4 on v3

--- a/solution.py
+++ b/solution.py
@@ -167,10 +167,12 @@
     wide_ref,
     force_ref,
     acc_ref,
+    sem_ref,
     *,
     capacity,
 ):
-    kept_ref[...] = rank_ref[...]
+    keep = pltpu.make_async_copy(rank_ref, kept_ref, sem_ref)
+    keep.start()
     units, _, unit = out_ref.shape
     width = acc_ref.shape[1]
     blocks = units * unit // width
@@ -202,10 +204,11 @@
         acc_ref[...] += fold(dot(spread(payload, block, blocks), one_hot(width, inside), NT))
         return carry
 
-    lax.fori_loop(0, markers // step, route, 0)
+    lax.fori_loop(0, markers // step, route, 0, unroll=8)
     for u in range(units):
         h, at = u * unit // width, u * unit % width
         out_ref[u] = acc_ref[8 * h : 8 * h + 8, at : at + unit]
+    keep.wait()
 
 
 def block_of(got_ref, i, per, capacity):
@@ -270,7 +273,7 @@
         acc_ref[...] += fold(dot(spread(payload, high, chunks), one_hot(LANES, low), NT))
         return carry
 
-    lax.fori_loop(0, sources // per, gather, 0)
+    lax.fori_loop(0, sources // per, gather, 0, unroll=4)
     for h in range(chunks):
         out_ref[h] = acc_ref[8 * h : 8 * h + 8]
 
@@ -287,7 +290,7 @@
             out_ref[i * per + j] = total[:, j * capacity : (j + 1) * capacity]
         return carry
 
-    lax.fori_loop(0, sources // per, scatter, 0)
+    lax.fori_loop(0, sources // per, scatter, 0, unroll=4)
 
 
 def basis_rows(x):
@@ -311,8 +314,10 @@
     hot = one_hot(GROUP, local.astype(jnp.bfloat16))
     for i, part in enumerate(split(basis_rows(payload[0:1]))):
         for a in range(POINTS):
-            row = jnp.broadcast_to(part[a : a + 1], (16, LANES)).astype(jnp.bfloat16)
-            weight_ref[i, a * GROUP : (a + 1) * GROUP, :] = hot * jnp.concatenate([row] * (GROUP // 16), axis=0)
+            row = jnp.broadcast_to(part[a : a + 1], (8, LANES))
+            row = jnp.concatenate([row, row], axis=0).astype(jnp.bfloat16)
+            for e in range(0, GROUP, 16):
+                weight_ref[i, a * GROUP + e : a * GROUP + e + 16, :] = hot[e : e + 16] * row
 
 
 def prepare_kernel(velocity_ref, out_ref):
@@ -328,8 +333,14 @@
             out_ref[g, half + k * side : half + (k + 1) * side, :] = low.astype(jnp.bfloat16)
 
 
-def total_of(wide, narrow):
-    half = narrow.shape[0]
+def product(left, weight_ref, dims, swap):
+    half = left.shape[0] // 2
+    if swap:
+        narrow = dot(left[:half], weight_ref[1], dims)
+        wide = dot(left, weight_ref[0], dims)
+    else:
+        wide = dot(left, weight_ref[0], dims)
+        narrow = dot(left[:half], weight_ref[1], dims)
     return wide[:half] + wide[half:] + narrow
 
 
@@ -342,7 +353,7 @@
     def several(i, carry):
         for j in range(depth):
             c = depth * i + j
-            visit(c, range_ref[0, c], weight_refs[j])
+            visit(c, range_ref[0, c], weight_refs[j], j % 2 == 1)
             ahead = jnp.minimum(c + depth, last)
             build_weights(sorted_ref[ahead], range_ref[0, ahead], weight_refs[j])
         return carry
@@ -371,11 +382,8 @@
     spans.wait()
     sampled_ref[...] = jnp.zeros_like(sampled_ref)
 
-    def visit(c, g, weight_ref):
-        half = velocity_ref.shape[1] // 2
-        wide = dot(velocity_ref[g], weight_ref[0], NN)
-        narrow = dot(velocity_ref[g, 0:half], weight_ref[1], NN)
-        total = total_of(wide, narrow)
+    def visit(c, g, weight_ref, swap):
+        total = product(velocity_ref[g], weight_ref, NN, swap)
         plane = plane_of(sorted_ref[c])
         side = plane.shape[0]
         sums = [jnp.sum(plane * total[k * side : (k + 1) * side], axis=0, keepdims=True) for k in range(3)]
@@ -388,14 +396,12 @@
 def deposit_kernel(range_ref, sorted_ref, out_ref, sum_ref, *weight_refs):
     sum_ref[...] = jnp.zeros_like(sum_ref)
 
-    def visit(c, g, weight_ref):
+    def visit(c, g, weight_ref, swap):
         payload = sorted_ref[c]
         plane = plane_of(payload)
         loads = jnp.concatenate([plane * payload[3 + k : 4 + k] for k in range(3)], axis=0)
         left = jnp.concatenate([part.astype(jnp.bfloat16) for part in split(loads)], axis=0)
-        wide = dot(left, weight_ref[0], NT)
-        narrow = dot(left[: loads.shape[0]], weight_ref[1], NT)
-        sum_ref[g] += total_of(wide, narrow)
+        sum_ref[g] += product(left, weight_ref, NT, swap)
 
     pipeline(range_ref, visit, sorted_ref, weight_refs)
     groups, rows, _ = sum_ref.shape
@@ -426,7 +432,7 @@
                 out_ref[k, row, :] = positions_ref[k, row, :] + time_step * part
         return carry
 
-    lax.fori_loop(0, owner_ref.shape[1] // step, chunk, 0)
+    lax.fori_loop(0, owner_ref.shape[1] // step, chunk, 0, unroll=8)
 
 
 def near(*arrays):
@@ -472,12 +478,13 @@
         functools.partial(pack_kernel, capacity=capacity),
         out_shape=(
             jax.ShapeDtypeStruct((slots // unit, 8, unit), f32),
-            jax.ShapeDtypeStruct((1, markers), f32),
+            pltpu.HBM((1, markers), f32),
         ),
         scratch_shapes=[
             pltpu.VMEM((4, rows + 16, columns), f32),
             pltpu.VMEM((3, rows, columns), f32),
             pltpu.VMEM((slots // width * 8, width), f32),
+            pltpu.SemaphoreType.DMA,
         ],
         compiler_params=SMALL,
         name="pack",

time: 73.9 us -> 67.7 us (0.916)
  the two profiles are of different devices: /device:TPU:1 before, /device:TPU:0 now
where the time goes in v4:
time: 67.7 us; the launch traced here: 66.6 us
  Pallas kernels  38.6 us (57%)
  waiting for transfers between devices  14.5 us (21%)
  starting transfers between devices  11.8 us (17%)
  other arithmetic  0.91 us (1%)
  between operations  0.74 us (1%)
    pallas_call x1, Pallas kernels, local(): pl.pallas_call(interpolate_kernel, out_shape=(pltpu.VMEM((devices, 4, cap...  16.4 us
    all_to_all x2, waiting for transfers between devices, exchange(): return lax.all_to_all(x, AXES, 0, 0, tiled=True)  10.3 us
    pallas_call x1, Pallas kernels, local(): pl.pallas_call(deposit_kernel, out_shape=jax.ShapeDtypeStruct(velocity.sh...  9.87 us
    ppermute x1, starting transfers between devices, halo(): lax.ppermute(head, AXES, [((i + 1) % count, i) for i in range(count)])  6.44 us
    all_to_all x2, starting transfers between devices, exchange(): return lax.all_to_all(x, AXES, 0, 0, tiled=True)  5.34 us
    pallas_call x1, Pallas kernels, local(): pl.pallas_call(functools.partial(pack_kernel, capacity=capacity), out_sha...  4.52 us
    ppermute x1, waiting for transfers between devices, halo(): lax.ppermute(tail, AXES, [(i, (i + 1) % count) for i in range(count)])  4.17 us
    pallas_call x1, Pallas kernels, local(): pl.pallas_call(prepare_kernel, out_shape=pltpu.VMEM((groups, 6 * side, PO...  2.92 us
  transfers between devices with their start and end apart: 4, of which 2 were waited for; matrix products, arithmetic and copies ran while one was open for 0% of the time, Pallas kernels for 23%

profile of v4, /device:TPU:0, one launch (start us, length us, event | category | flops | bytes accessed | tf_op | source)
XLA Modules:
  0.0 66.6 jit_solution(17819976842096970427)
XLA Ops:
  0.6 0.0 copy-start
  0.6 0.9 %pad_maximum_fusion = (f32[4,2,256]{2,1,0:T(2,128)S(1)}, f32[4,2,256]{2,1,0:T(2,128)S(1)}) fusion(f32[1,32,256]{2,1,0:T(8,128)} %bitcast.5, f32[3,32,256]{2,1,0:T(8,128)} %positions_ref.1), kind=kLoop, calls=%fused_computation | loop fusion | flops 4096 | bytes 147456 | tf_op jit(solution)/shard_map/concatenate | solution.py:45
  1.6 6.4 %collective-permute-start.1 = (f32[4,2,256]{2,1,0:T(2,128)S(1)}, f32[4,2,256]{2,1,0:T(2,128)S(1)}, u32[]{:S(2)}, u32[]{:S(2)}) collective-permute-start(f32[4,2,256]{2,1,0:T(2,128)S(1)} %get-tuple-element.26), channel_id=1, source_target_pairs={{1,0},{2,1},{3,2},{4,3},{5,4},{6,5},{7,6},{8,7},{9,8},{10,9},{11,1... | collective-permute-start | bytes 24584 | tf_op jit(solution)/shard_map/ppermute | solution.py:49
  8.0 0.0 collective-permute-start
  8.0 2.5 %rank.1 = (s32[1,8192]{1,0:T(1,128)S(1)}, s32[1,8192]{1,0:T(1,128)S(1)}, f32[3,8192]{1,0:T(4,128)S(1)}, f32[3,32,256]{2,1,0:T(8,128)S(1)}, f32[32,256]{1,0:T(8,1...) custom-call(s32[1,8192]{1,0:T(1,128)} %bitcast.3, s32[1,8192]{1,0:T(1,128)} %bitcast.6, f32[3,8192]{1,0:T(4,128)} %refs_2_.1, ...), custom_call_target="tpu_custom_call" | custom-call | tf_op jit(solution)/shard_map/rank/pallas_call | solution.py:465
  10.5 0.0 collective-permute-done.1.below_ref
  10.5 4.2 %collective-permute-done.above_ref = f32[4,2,256]{2,1,0:T(2,128)S(1)} collective-permute-done((f32[4,2,256]{2,1,0:T(2,128)S(1)}, f32[4,2,256]{2,1,0:T(2,128)S(1)}, u32[]{:S(2)}, u32[]{:S(2)}) %collective-permute-start) | collective-permute-done | bytes 8224 | tf_op jit(solution)/shard_map/ppermute | solution.py:48
  14.7 4.5 %pack.1 = (f32[96,8,128]{2,1,0:T(8,128)}, f32[1,8192]{1,0:T(1,128)}) custom-call(s32[1,8192]{1,0:T(1,128)S(1)} %get-tuple-element.14.owner_ref, s32[1,8192]{1,0:T(1,128)S(1)} %get-tuple-element.15.element_ref, f32[3,8192]{1,0:T(4,128)S(1)} %get-tuple-element.16.coords_ref, f32[3,32,256]{2,1,0:T(8,128)S(1)} %get-tuple-element.17.positions_ref, ...), custom_call_target="tpu_custom_call" | custom-call | tf_op jit(solution)/shard_map/pack/pallas_call | solution.py:477
  19.2 2.6 %all-to-all-start = ((f32[96,8,128]{2,1,0:T(8,128)}), f32[96,8,128]{2,1,0:T(8,128)S(1)}, u32[]{:S(2)}, u32[]{:S(2)}) async-start(f32[96,8,128]{2,1,0:T(8,128)} %get-tuple-element.22), calls=%async_computation | async-start | bytes 786432 | tf_op jit(solution)/shard_map/all_to_all | solution.py:447
  21.8 0.0 copy-done
  21.8 2.9 %prepare.1.velocity_ref = bf16[8,384,256]{2,1,0:T(8,128)(2,1)S(1)} custom-call(f32[3,256,512]{2,1,0:T(8,128)S(1)} %copy-done), custom_call_target="tpu_custom_call" | custom-call | tf_op jit(solution)/shard_map/prepare/pallas_call | solution.py:493
  24.7 10.3 %all-to-all-done.got_ref = f32[96,8,128]{2,1,0:T(8,128)S(1)} async-done(((f32[96,8,128]{2,1,0:T(8,128)}), f32[96,8,128]{2,1,0:T(8,128)S(1)}, u32[]{:S(2)}, u32[]{:S(2)}) %all-to-all-start) | async-done | bytes 393248 | tf_op jit(solution)/shard_map/all_to_all | solution.py:447
  35.1 16.4 %interpolate.1 = (f32[32,4,384]{2,1,0:T(4,128)}, f32[56,8,256]{2,1,0:T(8,128)S(1)}, s32[8,128]{1,0:T(8,128)S(1)}) custom-call(f32[96,8,128]{2,1,0:T(8,128)S(1)} %all-to-all-done.got_ref, bf16[8,384,256]{2,1,0:T(8,128)(2,1)S(1)} %prepare.1.velocity_ref), custom_call_target="tpu_custom_call" | custom-call | tf_op jit(solution)/shard_map/interpolate/pallas_call | solution.py:501
  51.4 0.0 copy-start.1
  51.5 0.0 copy-start.2
  51.5 0.0 copy-start.3
  51.5 2.7 %all-to-all-start.1 = ((f32[32,4,384]{2,1,0:T(4,128)}), f32[32,4,384]{2,1,0:T(4,128)S(1)}, u32[]{:S(2)}, u32[]{:S(2)}) async-start(f32[32,4,384]{2,1,0:T(4,128)} %get-tuple-element.23), calls=%async_computation.1 | async-start | bytes 393216 | tf_op jit(solution)/shard_map/all_to_all | solution.py:447
  54.2 9.9 %deposit.1 = f32[3,256,512]{2,1,0:T(8,128)} custom-call(s32[8,128]{1,0:T(8,128)S(1)} %get-tuple-element.24.range_ref, f32[56,8,256]{2,1,0:T(8,128)S(1)} %get-tuple-element.25.sorted_ref), custom_call_target="tpu_custom_call" | custom-call | tf_op jit(solution)/shard_map/deposit/pallas_call | solution.py:521
  64.1 0.0 all-to-all-done.1.arrived_ref
  64.1 0.0 copy-done.1
  64.1 0.0 copy-done.2
  64.1 0.0 copy-done.3
  64.1 2.5 %unpack.1 = f32[3,32,256]{2,1,0:T(8,128)} custom-call(s32[1,8192]{1,0:T(1,128)S(1)} %bitcast.4, f32[1,8192]{1,0:T(1,128)S(1)} %copy-done.3, f32[32,4,384]{2,1,0:T(4,128)S(1)} %all-to-all-done.1.arrived_ref, f32[3,32,256]{2,1,0:T(8,128)S(1)} %copy-done.1), custom_call_target="tpu_custom_call" | custom-call | tf_op jit(solution)/shard_map/unpack/pallas_call | solution.py:529
Async XLA Ops:
  0.6 21.2 %copy-start = (f32[3,256,512]{2,1,0:T(8,128)S(1)}, f32[3,256,512]{2,1,0:T(8,128)}, u32[]{:S(2)}) copy-start(f32[3,256,512]{2,1,0:T(8,128)} %velocity_ref.1) | copy-start | bytes 4718596
  1.6 8.9 %collective-permute-start.1 = (f32[4,2,256]{2,1,0:T(2,128)S(1)}, f32[4,2,256]{2,1,0:T(2,128)S(1)}, u32[]{:S(2)}, u32[]{:S(2)}) collective-permute-start(f32[4,2,256]{2,1,0:T(2,128)S(1)} %get-tuple-element.26), channel_id=1, source_target_pairs={{1,0},{2,1},{3,2},{4,3},{5,4},{6,5},{7,6},{8,7},{9,8},{10,9},{11,1... | collective-permute-start | bytes 24584 | tf_op jit(solution)/shard_map/ppermute | solution.py:49
  8.0 6.7 %collective-permute-start = (f32[4,2,256]{2,1,0:T(2,128)S(1)}, f32[4,2,256]{2,1,0:T(2,128)S(1)}, u32[]{:S(2)}, u32[]{:S(2)}) collective-permute-start(f32[4,2,256]{2,1,0:T(2,128)S(1)} %get-tuple-element.27), channel_id=1, source_target_pairs={{0,1},{1,2},{2,3},{3,4},{4,5},{5,6},{6,7},{7,8},{8,9},{9,10},{10,1... | collective-permute-start | bytes 24584 | tf_op jit(solution)/shard_map/ppermute | solution.py:48
  19.2 15.9 %all-to-all-start = ((f32[96,8,128]{2,1,0:T(8,128)}), f32[96,8,128]{2,1,0:T(8,128)S(1)}, u32[]{:S(2)}, u32[]{:S(2)}) async-start(f32[96,8,128]{2,1,0:T(8,128)} %get-tuple-element.22), calls=%async_computation | async-start | bytes 786432 | tf_op jit(solution)/shard_map/all_to_all | solution.py:447
  51.4 12.7 %copy-start.1 = (f32[3,32,256]{2,1,0:T(8,128)S(1)}, f32[3,32,256]{2,1,0:T(8,128)}, u32[]{:S(2)}) copy-start(f32[3,32,256]{2,1,0:T(8,128)} %positions_ref.1) | copy-start | bytes 294916
  51.5 12.6 %copy-start.2 = (s32[8192,1]{0,1:T(1,128)S(1)}, s32[8192,1]{0,1:T(1,128)}, u32[]{:S(2)}) copy-start(s32[8192,1]{0,1:T(1,128)} %param.11) | copy-start | bytes 98308
  51.5 12.6 %copy-start.3 = (f32[1,8192]{1,0:T(1,128)S(1)}, f32[1,8192]{1,0:T(1,128)}, u32[]{:S(2)}) copy-start(f32[1,8192]{1,0:T(1,128)} %get-tuple-element.21.rank_ref) | copy-start | bytes 98308
  51.5 12.6 %all-to-all-start.1 = ((f32[32,4,384]{2,1,0:T(4,128)}), f32[32,4,384]{2,1,0:T(4,128)S(1)}, u32[]{:S(2)}, u32[]{:S(2)}) async-start(f32[32,4,384]{2,1,0:T(4,128)} %get-tuple-element.23), calls=%async_computation.1 | async-start | bytes 393216 | tf_op jit(solution)/shard_map/all_to_all | solution.py:447
